TPU v7x, 8 devices: a whole 2x2x1 slice. The times are simulated.
8 devices in a mesh: dp: 1 (over z), tp: 8 (over y, x, core).
Axes of the slice: x: 2, y: 2, z: 1, core: 2. Of those that a mesh axis runs over, the one named last changes fastest.
Arguments:
- out_y1: float32 [32, 96, 4096], P('dp')
- out_y2: float32 [32, 96, 4096], P('dp')
- cot_y1: float32 [32, 96, 4096], P('dp')
- cot_y2: float32 [32, 96, 4096], P('dp')
- w_qkv: bfloat16 [1, 4096, 32, 3, 128], P(None, None, 'tp')
- w_out: bfloat16 [1, 32, 128, 4096], P(None, 'tp')
- w_up: bfloat16 [1, 4096, 16384], P(None, None, 'tp')
- w_down: bfloat16 [1, 16384, 4096], P(None, 'tp')
Outputs:
- output 1: float32 [32, 96, 4096], P('dp')
- output 2: float32 [32, 96, 4096], P('dp')
- output 3: float32 [32, 96, 4096], P('dp')
- output 4: float32 [32, 96, 4096], P('dp')
- output 5: float32 [1, 4096, 32, 3, 128], P('dp', None, 'tp')
- output 6: float32 [1, 32, 128, 4096], P('dp', 'tp')
- output 7: float32 [1, 4096, 16384], P('dp', None, 'tp')
- output 8: float32 [1, 16384, 4096], P('dp', 'tp')
All inputs are finite; a program needn't handle non-finite values.
Results may differ from a plain program's by a relative error of at most 0.0131098.
Values are sent between devices in bfloat16 or wider.
A program may use at most 2.25 GiB of HBM per device.

v0:
```python
import math
import jax
import jax.numpy as jnp
from jax import lax
from jax.sharding import PartitionSpec as P

NORM_EPS = 1e-6


def rms_fwd(x_in):
    inv_rms = lax.rsqrt(jnp.mean(x_in * x_in, axis=-1, keepdims=True) + NORM_EPS)
    return inv_rms, x_in * inv_rms


def rms_back(norm_state, grad_n):
    inv_rms, normed = norm_state
    return inv_rms * (grad_n - normed * jnp.mean(normed * grad_n, axis=-1, keepdims=True))


def mlp_forward(x_in, w_up, w_down):
    norm_state = rms_fwd(x_in)
    n_bf = norm_state[1].astype(jnp.bfloat16)
    hidden = jnp.einsum("bsd,df->bsf", n_bf, w_up, preferred_element_type=jnp.float32)
    act_f, gelu_back = jax.vjp(jax.nn.gelu, hidden)
    act_bf = act_f.astype(jnp.bfloat16)
    part_sum = jnp.einsum("bsf,fd->bsd", act_bf, w_down, preferred_element_type=jnp.float32)
    return part_sum, norm_state, (n_bf, act_bf, gelu_back)


def mlp_backward(cot_out, w_up, w_down, saved):
    n_bf, act_bf, gelu_back = saved
    cot_bf = cot_out.astype(jnp.bfloat16)
    g_down = jnp.einsum("bsf,bsd->fd", act_bf, cot_bf, preferred_element_type=jnp.float32)
    grad_act = jnp.einsum("bsd,fd->bsf", cot_bf, w_down, preferred_element_type=jnp.float32)
    grad_hid = gelu_back(grad_act)[0].astype(jnp.bfloat16)
    g_up = jnp.einsum("bsd,bsf->df", n_bf, grad_hid, preferred_element_type=jnp.float32)
    grad_n = jnp.einsum("bsf,df->bsd", grad_hid, w_up, preferred_element_type=jnp.float32)
    return g_up, g_down, grad_n


def attn_forward(x_in, w_qkv, w_out):
    norm_state = rms_fwd(x_in)
    n_bf = norm_state[1].astype(jnp.bfloat16)
    score_scale = 1.0 / math.sqrt(w_qkv.shape[-1])
    qkv = jnp.einsum("bsd,dhje->bshje", n_bf, w_qkv, preferred_element_type=jnp.float32).astype(jnp.bfloat16)
    q_rows = qkv[:, :, :, 0]
    k_rows = qkv[:, :, :, 1]
    v_rows = qkv[:, :, :, 2]
    scores = jnp.einsum("bqhe,bkhe->bhqk", q_rows, k_rows, preferred_element_type=jnp.float32) * score_scale
    attn_prob = jax.nn.softmax(scores, axis=-1)
    prob_bf = attn_prob.astype(jnp.bfloat16)
    attn_out = jnp.einsum("bhqk,bkhe->bqhe", prob_bf, v_rows, preferred_element_type=jnp.float32).astype(jnp.bfloat16)
    part_sum = jnp.einsum("crif,ife->cre", attn_out, w_out, preferred_element_type=jnp.float32)
    return part_sum, norm_state, (n_bf, q_rows, k_rows, v_rows, attn_prob, prob_bf, attn_out)


def attn_backward(cot_out, w_qkv, w_out, saved):
    n_bf, q_rows, k_rows, v_rows, attn_prob, prob_bf, attn_out = saved
    score_scale = 1.0 / math.sqrt(w_qkv.shape[-1])
    cot_bf = cot_out.astype(jnp.bfloat16)
    g_out = jnp.einsum("crif,cre->ife", attn_out, cot_bf, preferred_element_type=jnp.float32)
    grad_o = jnp.einsum("cre,ife->crif", cot_bf, w_out, preferred_element_type=jnp.float32).astype(jnp.bfloat16)
    grad_p = jnp.einsum("bqhe,bkhe->bhqk", grad_o, v_rows, preferred_element_type=jnp.float32)
    grad_v = jnp.einsum("bhqk,bqhe->bkhe", prob_bf, grad_o, preferred_element_type=jnp.float32)
    grad_s = (attn_prob * (grad_p - jnp.sum(grad_p * attn_prob, axis=-1, keepdims=True)) * score_scale).astype(jnp.bfloat16)
    grad_q = jnp.einsum("bhqk,bkhe->bqhe", grad_s, k_rows, preferred_element_type=jnp.float32)
    grad_k = jnp.einsum("bhqk,bqhe->bkhe", grad_s, q_rows, preferred_element_type=jnp.float32)
    grad_qkv = jnp.stack([grad_q, grad_k, grad_v], axis=3).astype(jnp.bfloat16)
    g_qkv = jnp.einsum("bsd,bshje->dhje", n_bf, grad_qkv, preferred_element_type=jnp.float32)
    grad_n = jnp.einsum("bshje,dhje->bsd", grad_qkv, w_qkv, preferred_element_type=jnp.float32)
    return g_qkv, g_out, grad_n


def solution(mesh):
    act_spec = P("dp", None, None)
    weight_specs = (P(None, None, "tp", None, None), P(None, "tp", None, None), P(None, None, "tp"), P(None, "tp", None))
    grad_specs = (P("dp", None, "tp", None, None), P("dp", "tp", None, None), P("dp", None, "tp"), P("dp", "tp", None))

    def local_backward(out_y1, out_y2, cot_y1, cot_y2, w_qkv, w_out, w_up, w_down):
        run_y1, run_y2, run_c1, run_c2 = out_y1, out_y2, cot_y1, cot_y2
        per_layer = []
        for layer_idx in reversed(range(w_qkv.shape[0])):
            g_part, g_norm, g_saved = mlp_forward(run_y1, w_up[layer_idx], w_down[layer_idx])
            low_x2 = run_y2 - lax.psum(g_part, "tp")
            g_up, g_down, gn_part = mlp_backward(run_c2, w_up[layer_idx], w_down[layer_idx], g_saved)
            grad_n = lax.psum(gn_part.astype(jnp.bfloat16), "tp").astype(jnp.float32)
            run_c1 = run_c1 + rms_back(g_norm, grad_n)
            f_part, f_norm, f_saved = attn_forward(low_x2, w_qkv[layer_idx], w_out[layer_idx])
            run_y1 = run_y1 - lax.psum(f_part, "tp")
            g_qkv, g_out, fn_part = attn_backward(run_c1, w_qkv[layer_idx], w_out[layer_idx], f_saved)
            grad_n = lax.psum(fn_part.astype(jnp.bfloat16), "tp").astype(jnp.float32)
            run_c2 = run_c2 + rms_back(f_norm, grad_n)
            run_y2 = low_x2
            per_layer.append((g_qkv, g_out, g_up, g_down))
        per_layer = per_layer[::-1]
        stacked = [jnp.stack([layer_grads[slot_idx] for layer_grads in per_layer]) for slot_idx in range(4)]
        return (run_y1, run_y2, run_c1, run_c2, stacked[0], stacked[1], stacked[2], stacked[3])

    return jax.shard_map(local_backward, mesh=mesh, in_specs=(act_spec, act_spec, act_spec, act_spec) + weight_specs, out_specs=(act_spec, act_spec, act_spec, act_spec) + grad_specs, check_vma=False)
```

profile of v0, /device:TPU:0, one launch (start us, length us, event | category | flops | bytes accessed | tf_op | source)
XLA Modules:
  0.0 2172.3 jit_solution(2577519704518829142)
XLA Ops:
  7.2 0.0 all-reduce.5.cloned.1.call-start
  7.2 18.0 multiply_reduce_fusion.1
  25.3 0.0 copy-start.3
  25.3 63.3 %fusion.28 = f32[32,96,2048]{2,1,0:T(8,128)} fusion(bf16[1,4096,2048]{2,1,0:T(8,128)(2,1)} %param.14, f32[32,96,4096]{2,1,0:T(8,128)} %param.8, f32[32,96]{1,0:T(8,128)S(1)} %add_rsqrt_fusion.1), kind=kOutput, calls=%fused_computation.43 | convolution fusion | flops 51564773376 | bytes 92286976 | tf_op jit(solution)/shard_map/bsd,df->bsf/dot_general | solution.py:23
  88.6 0.0 copy-done.3
  88.6 65.4 %fusion.24 = f32[32,96,4096]{2,1,0:T(8,128)} fusion(bf16[1,2048,4096]{2,1,0:T(8,128)(2,1)} %param.15, f32[32,96,2048]{2,1,0:T(8,128)} %fusion.28), kind=kOutput, calls=%fused_computation.39 | convolution fusion | flops 51596230656 | bytes 92274688 | tf_op jit(solution)/shard_map/bsf,fd->bsd/dot_general | solution.py:26
  154.0 0.0 all-reduce.5.cloned.1.call-update
  154.0 0.2 all-reduce.9.cloned.1.call-start
  154.2 76.0 %fusion.14 = bf16[32,96,2048]{2,1,0:T(8,128)(2,1)} fusion(f32[32,96,2048]{2,1,0:T(8,128)} %fusion.28, bf16[1,2048,4096]{2,1,0:T(8,128)(2,1)} %param.15, f32[32,96,4096]{2,1,0:T(8,128)} %param.11), kind=kOutput, calls=%fused_computation.25 | convolution fusion | flops 51678019584 | bytes 104857600 | tf_op jit(solution)/shard_map/bsd,fd->bsf/dot_general | solution.py:34
  230.2 61.0 %fusion.30 = bf16[32,96,4096]{2,1,0:T(8,128)(2,1)} fusion(bf16[32,96,2048]{2,1,0:T(8,128)(2,1)} %fusion.14, bf16[1,4096,2048]{2,1,0:T(8,128)(2,1)} %param.14), kind=kOutput, calls=%fused_computation.45 | convolution fusion | flops 51552190464 | bytes 54525952 | tf_op jit(solution)/shard_map/bsf,df->bsd/dot_general | solution.py:37
  291.2 0.0 all-reduce.9.cloned.1.call-update
  291.2 0.4 all-reduce.7.cloned.1.call-start
  291.6 432.5 %all-reduce.5.cloned.1.call-done = f32[32,96,4096]{2,1,0:T(8,128)} async-done(((f32[32,96,4096]{2,1,0:T(8,128)}), f32[32,96,4096]{2,1,0:T(8,128)}) %all-reduce.5.cloned.1.call-update) | async-done | bytes 50331664 | tf_op jit(solution)/shard_map/psum | solution.py:84
  724.2 48.9 %multiply_reduce_fusion = (f32[32,96]{1,0:T(8,128)S(1)}, f32[32,96,4096]{2,1,0:T(8,128)}) fusion(f32[32,96,4096]{2,1,0:T(8,128)} %param.9, f32[32,96,4096]{2,1,0:T(8,128)} %all-reduce.5.cloned.1.call-done), kind=kLoop, calls=%fused_computation.13 | loop fusion | flops 37745664 | bytes 151007232 | tf_op jit(solution)/shard_map/reduce_sum | solution.py:11
  773.1 0.0 copy-start.1
  773.1 48.5 %fusion.44 = bf16[32,96,4,3,128]{4,1,3,2,0:T(8,128)(2,1)} fusion(bf16[4096,4,3,128]{3,1,2,0:T(4,128)(2,1)} %bitcast.125, f32[32,96,4096]{2,1,0:T(8,128)} %get-tuple-element.17, f32[32,96]{1,0:T(8,128)S(1)} %add_rsqrt_fusion), kind=kOutput, calls=%fused_computation.56 | convolution fusion | flops 38684590080 | bytes 72364032 | tf_op jit(solution)/shard_map/bsd,dhje->bshje/dot_general | solution.py:45
  821.6 0.0 copy-done.1
  821.6 5.1 fusion.73
  826.7 0.0 copy-start.7
  826.7 7.2 fusion.91
  833.8 0.0 copy-start
  833.9 0.0 copy-start.5
  833.9 2.7 copy-done
  836.6 3.2 fusion.74
  839.7 0.0 copy-done.5
  839.7 0.0 copy-start.9
  839.8 1.6 copy-done.9
  841.4 0.0 copy-done.7
  841.4 20.0 convolution_bitcast_fusion.2
  861.4 0.0 copy-start.4
  861.4 0.0 all-reduce.7.cloned.1.call-update
  861.4 0.2 all-reduce.11.cloned.1.call-start
  861.6 0.5 copy-done.4
  862.1 64.3 %convolution_bitcast_fusion.1 = f32[1,4096,2048]{2,1,0:T(8,128)} fusion(bf16[32,96,2048]{2,1,0:T(8,128)(2,1)} %fusion.14, f32[32,96,4096]{2,1,0:T(8,128)} %param.8, f32[32,96]{1,0:T(8,128)S(1)} %copy-done.4), kind=kOutput, calls=%fused_computation.36 | convolution fusion | flops 51564773376 | bytes 96481280 | tf_op jit(solution)/shard_map/bsd,bsf->df/dot_general | solution.py:36
  926.4 85.0 %convolution_bitcast_fusion = f32[1,2048,4096]{2,1,0:T(8,128)} fusion(f32[32,96,4096]{2,1,0:T(8,128)} %param.11, f32[32,96,2048]{2,1,0:T(8,128)} %fusion.28), kind=kOutput, calls=%fused_computation.35 | convolution fusion | flops 51608813568 | bytes 109051904 | tf_op jit(solution)/shard_map/bsf,bsd->fd/dot_general | solution.py:33
  1011.4 12.4 all-reduce.9.cloned.1.call-done
  1023.7 23.6 %fusion.2 = f32[32,96]{1,0:T(8,128)S(1)} fusion(bf16[32,96,4096]{2,1,0:T(8,128)(2,1)} %all-reduce.9.cloned.1.call-done, f32[32,96,4096]{2,1,0:T(8,128)} %param.8, f32[32,96]{1,0:T(8,128)S(1)} %copy-done.4), kind=kLoop, calls=%fused_computation.6 | loop fusion | flops 50328576 | bytes 75522048 | tf_op jit(solution)/shard_map/reduce_sum | solution.py:17
  1047.3 548.0 %all-reduce.7.cloned.1.call-done = f32[32,96,4096]{2,1,0:T(8,128)} async-done(((f32[32,96,4096]{2,1,0:T(8,128)}), f32[32,96,4096]{2,1,0:T(8,128)}) %all-reduce.7.cloned.1.call-update) | async-done | bytes 50331664 | tf_op jit(solution)/shard_map/psum | solution.py:89
  1595.4 0.0 copy-start.8
  1595.4 87.9 %fusion.4 = (f32[32,96,4096]{2,1,0:T(8,128)}, f32[32,96,4096]{2,1,0:T(8,128)}) fusion(f32[32,96,4096]{2,1,0:T(8,128)} %param.10, bf16[32,96,4096]{2,1,0:T(8,128)(2,1)} %all-reduce.9.cloned.1.call-done, f32[32,96,4096]{2,1,0:T(8,128)} %param.8, f32[32,96]{1,0:T(8,128)S(1)} %broadcast_multiply_fusion.1, f32[32,96]{1,0:T(8,128)S(1)} %copy-done.4, ...), kind=kLoop, calls=%fused_computation.8 | loop fusion | flops 88080384 | bytes 276848640 | tf_op jit(solution)/shard_map/add | solution.py:87
  1683.3 0.0 copy-done.8
  1683.3 0.0 copy-start.6
  1683.3 20.5 fusion.79
  1703.8 6.8 fusion.71
  1710.6 0.0 copy-done.6
  1710.6 13.0 convert_bitcast_fusion.2
  1723.6 13.3 convert_bitcast_fusion.1
  1736.9 5.4 convert_bitcast_fusion
  1742.3 47.5 %bitcast_convert_fusion = bf16[32,96,4096]{2,1,0:T(8,128)(2,1)} fusion(bf16[4096,4,3,128,1]{3,1,2,0,4:T(4,128)(2,1)} %bitcast.126, bf16[32,96,4,1,128]{4,1,2,0,3:T(8,128)(2,1)} %convert_bitcast_fusion, bf16[32,96,4,1,128]{4,1,2,0,3:T(8,128)(2,1)} %convert_bitcast_fusion.1, bf16[32,96,4,1,128]{4,1,2,0,3:T(8,128)(2,1)} %convert_bitcast_fusion.2), kind=kOutput, calls=%fused_computation.12 | convolution fusion | flops 38676725760 | bytes 47185920 | tf_op jit(solution)/shard_map/bshje,dhje->bsd/dot_general | solution.py:70
  1789.8 0.0 copy-start.2
  1789.8 0.0 copy-start.11
  1789.8 0.0 all-reduce.11.cloned.1.call-update
  1789.8 0.7 copy-done.2
  1790.5 1.2 copy-done.11
  1791.7 50.0 %fusion.40 = f32[1,4096,4,3,128]{4,1,3,2,0:T(8,128)} fusion(f32[32,96,4096]{2,1,0:T(8,128)} %get-tuple-element.17, f32[32,96]{1,0:T(8,128)S(1)} %copy-done.2, bf16[32,96,4,1,128]{4,1,2,0,3:T(8,128)(2,1)S(1)} %copy-done.11, bf16[32,96,4,1,128]{4,1,2,0,3:T(8,128)(2,1)} %convert_bitcast_fusion.1, bf16[32,96,4,1,128]{4,1,2,0,3:T(8,128)(2,1)} %convert_bitcast_fusion.2), kind=kOutput, calls=%fused_computation.53 | convolution fusion | flops 38689308672 | bytes 84946944 | tf_op jit(solution)/shard_map/bsd,bshje->dhje/dot_general | solution.py:69
  1841.6 0.0 copy-start.10
  1841.6 30.1 %copy.23 = f32[1,4096,4,3,128]{4,2,3,1,0:T(4,128)} copy(f32[1,4096,4,3,128]{4,1,3,2,0:T(8,128)} %fusion.40) | data formatting | bytes 50331648
  1871.8 0.0 copy-done.10
  1871.8 24.4 %fusion.49 = f32[1,4,128,4096]{3,2,1,0:T(8,128)} fusion(f32[32,96,4096]{2,1,0:T(8,128)} %get-tuple-element.18, bf16[32,4,128,96]{2,3,1,0:T(8,128)(2,1)S(1)} %copy-done.10), kind=kOutput, calls=%fused_computation.57 | convolution fusion | flops 12897484800 | bytes 61865984 | tf_op jit(solution)/shard_map/crif,cre->ife/dot_general | solution.py:61
  1896.2 189.0 %all-reduce.11.cloned.1.call-done = bf16[32,96,4096]{2,1,0:T(8,128)(2,1)} async-done(((bf16[32,96,4096]{2,1,0:T(8,128)(2,1)}), bf16[32,96,4096]{2,1,0:T(8,128)(2,1)}) %all-reduce.11.cloned.1.call-update) | async-done | bytes 25165840 | tf_op jit(solution)/shard_map/psum | solution.py:91
  2085.2 23.6 %fusion.5 = f32[32,96]{1,0:T(8,128)S(1)} fusion(bf16[32,96,4096]{2,1,0:T(8,128)(2,1)} %all-reduce.11.cloned.1.call-done, f32[32,96,4096]{2,1,0:T(8,128)} %get-tuple-element.17, f32[32,96]{1,0:T(8,128)S(1)} %copy-done.2), kind=kLoop, calls=%fused_computation.9 | loop fusion | flops 50328576 | bytes 75522048 | tf_op jit(solution)/shard_map/reduce_sum | solution.py:17
  2108.8 56.7 %fusion.7 = f32[32,96,4096]{2,1,0:T(8,128)} fusion(f32[32,96,4096]{2,1,0:T(8,128)} %param.11, bf16[32,96,4096]{2,1,0:T(8,128)(2,1)} %all-reduce.11.cloned.1.call-done, f32[32,96,4096]{2,1,0:T(8,128)} %get-tuple-element.17, f32[32,96]{1,0:T(8,128)S(1)} %broadcast_multiply_fusion, f32[32,96]{1,0:T(8,128)S(1)} %copy-done.2), kind=kLoop, calls=%fused_computation.11 | loop fusion | flops 75497472 | bytes 176185344 | tf_op jit(solution)/shard_map/add | solution.py:92
  (4 shorter events, 0.0 us)
Async XLA Ops:
  7.2 717.0 %all-reduce.5.cloned.1.call-start = ((), (), s32[]{:S(2)}) async-start(), calls=%async_computation | async-start | bytes 100663296 | tf_op jit(solution)/shard_map/psum | solution.py:84
  25.3 63.3 %copy-start.3 = (f32[32,96]{1,0:T(8,128)}, f32[32,96]{1,0:T(8,128)S(1)}, u32[]{:S(2)}) copy-start(f32[32,96]{1,0:T(8,128)S(1)} %add_rsqrt_fusion.1) | copy-start | bytes 36868
  154.0 869.7 %all-reduce.9.cloned.1.call-start = ((), (), s32[]{:S(2)}) async-start(), calls=%async_computation.2 | async-start | bytes 50331648 | tf_op jit(solution)/shard_map/psum | solution.py:86
  291.2 1304.2 %all-reduce.7.cloned.1.call-start = ((), (), s32[]{:S(2)}) async-start(), calls=%async_computation.1 | async-start | bytes 100663296 | tf_op jit(solution)/shard_map/psum | solution.py:89
  773.1 48.5 %copy-start.1 = (f32[32,96]{1,0:T(8,128)}, f32[32,96]{1,0:T(8,128)S(1)}, u32[]{:S(2)}) copy-start(f32[32,96]{1,0:T(8,128)S(1)} %add_rsqrt_fusion) | copy-start | bytes 36868
  826.7 14.8 copy-start.7
  833.8 2.7 copy-start
  833.9 5.9 copy-start.5
  839.7 1.7 copy-start.9
  861.4 0.7 copy-start.4
  861.4 1223.8 %all-reduce.11.cloned.1.call-start = ((), (), s32[]{:S(2)}) async-start(), calls=%async_computation.3 | async-start | bytes 50331648 | tf_op jit(solution)/shard_map/psum | solution.py:91
  1595.4 87.9 %copy-start.8 = (bf16[1,4,128,4096]{3,2,1,0:T(8,128)(2,1)S(1)}, bf16[1,4,128,4096]{3,2,1,0:T(8,128)(2,1)}, u32[]{:S(2)}) copy-start(bf16[1,4,128,4096]{3,2,1,0:T(8,128)(2,1)} %param.13) | copy-start | bytes 12582916
  1683.3 27.3 %copy-start.6 = (f32[32,4,96]{2,1,0:T(4,128)S(1)}, f32[32,4,96]{2,1,0:T(4,128)}, u32[]{:S(2)}) copy-start(f32[32,4,96]{2,1,0:T(4,128)} %copy-done.5) | copy-start | bytes 147460
  1789.8 0.7 copy-start.2
  1789.8 1.9 copy-start.11
  1841.6 30.2 %copy-start.10 = (bf16[32,4,128,96]{2,3,1,0:T(8,128)(2,1)S(1)}, bf16[32,4,128,96]{2,3,1,0:T(8,128)(2,1)}, u32[]{:S(2)}) copy-start(bf16[32,4,128,96]{2,3,1,0:T(8,128)(2,1)} %copy-done.9) | copy-start | bytes 9437188
Sparse Core Ops, SparseCore 0:
  154.1 570.0 all-reduce.4
  728.4 295.2 all-reduce.8
  1028.1 567.2 all-reduce.6
  1789.9 295.2 all-reduce.10
where the time goes:
time: 2180 us; the launch traced here: 2170 us
  waiting for transfers between devices  1180 us (54%)
  matrix products  672 us (31%)
  other arithmetic  266 us (12%)
  local copies, waits for them, and re-layouts  36.9 us (2%)
    psum x1, waiting for transfers between devices, local_backward(): run_y1 = run_y1 - lax.psum(f_part, 'tp')  548 us
    psum x1, waiting for transfers between devices, local_backward(): low_x2 = run_y2 - lax.psum(g_part, 'tp')  433 us
    psum x1, waiting for transfers between devices, local_backward(): grad_n = lax.psum(fn_part.astype(jnp.bfloat16), 'tp').astype(jnp.float32)  189 us
    add x1, other arithmetic, local_backward(): run_c1 = run_c1 + rms_back(g_norm, grad_n)  87.9 us
    dot_general x1, matrix products, mlp_backward(): jnp.einsum('bsf,bsd->fd', act_bf, cot_bf, preferred_element_type=jnp.floa...  85 us
    dot_general x1, matrix products, mlp_backward(): jnp.einsum('bsd,fd->bsf', cot_bf, w_down, preferred_element_type=jnp.floa...  76 us
    reduce_sum x2, other arithmetic, rms_fwd(): jnp.mean(x_in * x_in, axis=-1, keepdims=True) + NORM_EPS  66.9 us
    dot_general x1, matrix products, mlp_forward(): jnp.einsum('bsf,fd->bsd', act_bf, w_down, preferred_element_type=jnp.floa...  65.4 us
  transfers between devices with their start and end apart: 4, of which 4 were waited for; matrix products, arithmetic and copies ran while one was open for 25% of the time, Pallas kernels for 0%

commit v1 on v0

v1 whole, which is shorter than its diff:
```python
import functools
import math
import jax
import jax.numpy as jnp
from jax import lax
from jax.experimental import pallas as pl
from jax.sharding import PartitionSpec as P


NORM_EPS = 1e-6
ROW_BLOCK = 128
SEQ_BLOCK = 2
F32 = jnp.float32
BF16 = jnp.bfloat16


def dot(lhs, rhs, lhs_dim, rhs_dim):
    return lax.dot_general(lhs, rhs, (((lhs_dim,), (rhs_dim,)), ((), ())), preferred_element_type=F32)


def rms_kernel(x_ref, n_ref, *copy_ref):
    x_in = x_ref[...]
    inv_rms = lax.rsqrt(jnp.mean(x_in * x_in, axis=-1, keepdims=True) + NORM_EPS)
    n_ref[...] = (x_in * inv_rms).astype(BF16)
    for ref in copy_ref:
        ref[...] = x_in


def rms_rows(x_in, with_copy):
    rows, width = x_in.shape
    spec = pl.BlockSpec((ROW_BLOCK, width), lambda i: (i, 0))
    shapes = [jax.ShapeDtypeStruct(x_in.shape, BF16)] + [jax.ShapeDtypeStruct(x_in.shape, F32)] * with_copy
    return pl.pallas_call(
        rms_kernel,
        grid=(rows // ROW_BLOCK,),
        in_specs=[spec],
        out_specs=[spec] * len(shapes),
        out_shape=shapes,
        cost_estimate=pl.CostEstimate(flops=rows * width * 256, bytes_accessed=rows * width * 6, transcendentals=0),
        name="rms_rows",
    )(x_in)


def rms_back_kernel(x_ref, grad_ref, cot_ref, out_ref, *bf_ref):
    x_in = x_ref[...]
    grad_n = grad_ref[...].astype(F32)
    inv_rms = lax.rsqrt(jnp.mean(x_in * x_in, axis=-1, keepdims=True) + NORM_EPS)
    normed = x_in * inv_rms
    inner = jnp.mean(normed * grad_n, axis=-1, keepdims=True)
    total = cot_ref[...] + inv_rms * (grad_n - normed * inner)
    out_ref[...] = total
    for ref in bf_ref:
        ref[...] = total.astype(BF16)


def rms_back_rows(x_in, grad_n, cot, with_bf16):
    rows, width = x_in.shape
    spec = pl.BlockSpec((ROW_BLOCK, width), lambda i: (i, 0))
    shapes = [jax.ShapeDtypeStruct(x_in.shape, F32)] + [jax.ShapeDtypeStruct(x_in.shape, BF16)] * with_bf16
    return pl.pallas_call(
        rms_back_kernel,
        grid=(rows // ROW_BLOCK,),
        in_specs=[spec] * 3,
        out_specs=[spec] * len(shapes),
        out_shape=shapes,
        cost_estimate=pl.CostEstimate(flops=rows * width * 512, bytes_accessed=rows * width * 16, transcendentals=0),
        name="rms_back_rows",
    )(x_in, grad_n, cot)


def head_probs(qkv_ref, rows, col, head):
    q_rows, k_rows, v_rows = (qkv_ref[rows, pl.ds(col + part * head, head)] for part in range(3))
    scores = dot(q_rows, k_rows, 1, 1) * (1.0 / math.sqrt(head))
    unnorm = jnp.exp(scores - jnp.max(scores, axis=-1, keepdims=True))
    return q_rows, k_rows, v_rows, unnorm / jnp.sum(unnorm, axis=-1, keepdims=True)


def attn_fwd_kernel(seq, head, qkv_ref, out_ref):
    for start in range(0, qkv_ref.shape[0], seq):
        rows = pl.ds(start, seq)
        for idx in range(out_ref.shape[1] // head):
            _, _, v_rows, prob = head_probs(qkv_ref, rows, 3 * head * idx, head)
            out_ref[rows, pl.ds(idx * head, head)] = dot(prob.astype(BF16), v_rows, 1, 0).astype(BF16)


def attn_back_kernel(seq, head, qkv_ref, grad_o_ref, grad_ref):
    for start in range(0, qkv_ref.shape[0], seq):
        rows = pl.ds(start, seq)
        for idx in range(grad_o_ref.shape[1] // head):
            col = 3 * head * idx
            q_rows, k_rows, v_rows, prob = head_probs(qkv_ref, rows, col, head)
            grad_o = grad_o_ref[rows, pl.ds(idx * head, head)]
            grad_p = dot(grad_o, v_rows, 1, 1)
            inner = jnp.sum(grad_p * prob, axis=-1, keepdims=True)
            grad_s = (prob * (grad_p - inner) * (1.0 / math.sqrt(head))).astype(BF16)
            grads = (dot(grad_s, k_rows, 1, 0), dot(grad_s, q_rows, 0, 0), dot(prob.astype(BF16), grad_o, 0, 0))
            for part, grad in enumerate(grads):
                grad_ref[rows, pl.ds(col + part * head, head)] = grad.astype(BF16)


def attn_call(kernel, seq, head, out_cols, *arrays):
    rows = arrays[0].shape[0]
    block = SEQ_BLOCK * seq
    spec = lambda cols: pl.BlockSpec((block, cols), lambda i: (i, 0))
    return pl.pallas_call(
        functools.partial(kernel, seq, head),
        grid=(rows // block,),
        in_specs=[spec(array.shape[1]) for array in arrays],
        out_specs=spec(out_cols),
        out_shape=jax.ShapeDtypeStruct((rows, out_cols), BF16),
        cost_estimate=pl.CostEstimate(flops=rows * 3072 * 2048, bytes_accessed=rows * 4096, transcendentals=0),
    )(*arrays)


def solution(mesh):
    n_tp = mesh.shape["tp"]
    act_spec = P("dp", None, None)
    weight_specs = (P(None, None, "tp", None, None), P(None, "tp", None, None), P(None, None, "tp"), P(None, "tp", None))
    grad_specs = (P("dp", None, "tp", None, None), P("dp", "tp", None, None), P("dp", None, "tp"), P("dp", "tp", None))
    partner = [(i, i ^ 1) for i in range(n_tp)]
    chips = [[i for i in range(n_tp) if i % 2 == core] for core in range(2)]

    def halves(rows_in):
        core = lax.rem(lax.axis_index("tp"), 2)
        blocks = rows_in.reshape(n_tp // 2, 2, rows_in.shape[0] // n_tp, rows_in.shape[1])
        pick = lambda which: lax.dynamic_index_in_dim(blocks, which, 1, keepdims=False).reshape(-1, rows_in.shape[1])
        return pick(core), pick(1 - core)

    def scatter_product(lhs, rhs, rhs_dim, travel, fill, behind=(), after=()):
        keep, send = halves(lhs)
        send, after = lax.optimization_barrier((send, after))
        got = lax.ppermute(dot(send, rhs, 1, rhs_dim).astype(travel), "tp", partner)
        keep, fill = lax.optimization_barrier((keep, fill))
        chip_sum = (dot(keep, rhs, 1, rhs_dim) + got.astype(F32)).astype(travel)
        chip_sum, fill, behind = lax.optimization_barrier((chip_sum, fill, behind))
        own = lax.psum_scatter(chip_sum, "tp", scatter_dimension=0, tiled=True, axis_index_groups=chips)
        return own, fill, behind, after

    def gather(shard):
        return lax.all_gather(shard, "tp", axis=0, tiled=True)

    def layer(run_y1, run_y2, run_c1, run_c2, w_qkv, w_out, w_up, w_down, seqs):
        rows, width = run_y1.shape
        heads, head = w_qkv.shape[1], w_qkv.shape[3]
        wq_mat = w_qkv.reshape(width, heads * 3 * head)
        wo_mat = w_out.reshape(heads * head, width)
        wo_all = gather(wo_mat).reshape(n_tp, heads * head, width)

        (n1,) = rms_rows(run_y1, False)
        hidden = dot(n1, w_up, 1, 0)
        act_f, gelu_back = jax.vjp(jax.nn.gelu, hidden)
        act_bf = act_f.astype(BF16)
        c2_bf = run_c2.astype(BF16)
        g_own, c2_bf, wo_all, _ = scatter_product(act_bf, w_down, 0, F32, c2_bf, wo_all)
        own_at = lax.axis_index("tp") * (rows // n_tp)
        x2_own = lax.dynamic_slice_in_dim(run_y2, own_at, rows // n_tp, 0) - g_own

        grad_hid = gelu_back(dot(c2_bf, w_down, 1, 1))[0].astype(BF16)
        gn_own = scatter_product(grad_hid, w_up, 1, BF16, ())[0]
        x2 = gather(x2_own)
        gn = gather(gn_own)
        g_down = dot(act_bf, c2_bf, 0, 0)
        g_up = dot(n1, grad_hid, 0, 0)

        x2, g_down, g_up = lax.optimization_barrier((x2, g_down, g_up))
        n2, x2_out = rms_rows(x2, True)
        qkv = dot(n2, wq_mat, 1, 0).astype(BF16)
        attn_out = attn_call(attn_fwd_kernel, rows // seqs, head, heads * head, qkv)
        attn_out, gn = lax.optimization_barrier((attn_out, gn))
        c1, c1_bf = rms_back_rows(run_y1, gn, run_c1, True)
        o_all = lax.all_gather(attn_out, "tp", axis=0)
        g_out = dot(attn_out, c1_bf, 0, 0).reshape(w_out.shape)

        grad_o = dot(c1_bf, wo_mat, 1, 1).astype(BF16)
        grad_qkv = attn_call(attn_back_kernel, rows // seqs, head, heads * 3 * head, qkv, grad_o)
        fn_own, g_out, _, o_all = scatter_product(grad_qkv, wq_mat, 1, BF16, g_out, (), o_all)
        x1 = run_y1 - jnp.einsum("jtk,jkd->td", o_all, wo_all, preferred_element_type=F32)
        fn_own, x1 = lax.optimization_barrier((fn_own, x1))
        fn = gather(fn_own)
        g_qkv = dot(n2, grad_qkv, 0, 0).reshape(w_qkv.shape)
        (c2,) = rms_back_rows(x2, fn, run_c2, False)
        return x1, x2_out, c1, c2, g_qkv, g_out, g_up, g_down

    def local_backward(out_y1, out_y2, cot_y1, cot_y2, w_qkv, w_out, w_up, w_down):
        seqs, width = out_y1.shape[0], out_y1.shape[2]
        state = tuple(array.reshape(-1, width) for array in (out_y1, out_y2, cot_y1, cot_y2))
        per_layer = []
        for idx in reversed(range(w_qkv.shape[0])):
            result = layer(*state, w_qkv[idx], w_out[idx], w_up[idx], w_down[idx], seqs)
            state = result[:4]
            per_layer.insert(0, result[4:])
        stacked = tuple(jnp.stack(slot) for slot in zip(*per_layer))
        return tuple(array.reshape(out_y1.shape) for array in state) + stacked

    return jax.shard_map(local_backward, mesh=mesh, in_specs=(act_spec,) * 4 + weight_specs, out_specs=(act_spec,) * 4 + grad_specs, check_vma=False)
```

time: 2180 us -> 1500 us (0.69)
  waiting for transfers between devices: 1180 us -> 278 us
  Pallas kernels: 0 us -> 328 us
  other arithmetic: 266 us -> 34.8 us
  local copies, waits for them, and re-layouts: 36.9 us -> 116 us
  matrix products: 672 us -> 718 us
    psum x4 -> x0, waiting for transfers between devices: 1180 us -> none  [the longest x1 548 us: local_backward(): run_y1 = run_y1 - lax.psum(f_part, 'tp')]
    pallas_call x0 -> x6, Pallas kernels: none -> 328 us  [the longest x2 141 us: rms_back_rows(): pl.pallas_call(rms_back_kernel, grid=(rows // ROW_BLOCK,), in_specs=[spec...]
    reduce_scatter x0 -> x3, waiting for transfers between devices: none -> 157 us  [scatter_product(): lax.psum_scatter(chip_sum, 'tp', scatter_dimension=0, tiled=True, axis_in...]
    add x2 -> x0, other arithmetic: 145 us -> none  [the longest x1 87.9 us: local_backward(): run_c1 = run_c1 + rms_back(g_norm, grad_n)]
    reduce_sum x4 -> x0, other arithmetic: 114 us -> none  [the longest x2 66.9 us: rms_fwd(): jnp.mean(x_in * x_in, axis=-1, keepdims=True) + NORM_EPS]
    all_gather x0 -> x5, waiting for transfers between devices: none -> 87.5 us  [the longest x4 87.5 us: gather(): return lax.all_gather(shard, 'tp', axis=0, tiled=True)]
    unnamed x25 -> x9, local copies, waits for them, and re-layouts: 36.9 us -> 83.6 us
    dot_general x18 -> x15, matrix products: 672 us -> 718 us  [the longest x14 601 us: dot(): lax.dot_general(lhs, rhs, (((lhs_dim,), (rhs_dim,)), ((), ())), preferred...]
  transfers between devices with their start and end apart: 4 -> 11, of which waited for: 4 -> 7; matrix products, arithmetic and copies ran while one was open for 25% -> 55% of each run, Pallas kernels for 0% -> 18%
where the time goes in v1:
time: 1500 us; the launch traced here: 1490 us
  matrix products  718 us (48%)
  Pallas kernels  328 us (22%)
  waiting for transfers between devices  278 us (19%)
  local copies, waits for them, and re-layouts  116 us (8%)
  other arithmetic  34.8 us (2%)
    dot_general x14, matrix products, dot(): lax.dot_general(lhs, rhs, (((lhs_dim,), (rhs_dim,)), ((), ())), preferred...  601 us
    reduce_scatter x3, waiting for transfers between devices, scatter_product(): lax.psum_scatter(chip_sum, 'tp', scatter_dimension=0, tiled=True, axis_in...  157 us
    pallas_call x2, Pallas kernels, rms_back_rows(): pl.pallas_call(rms_back_kernel, grid=(rows // ROW_BLOCK,), in_specs=[spec...  141 us
    dot_general x1, matrix products, layer(): jnp.einsum('jtk,jkd->td', o_all, wo_all, preferred_element_type=F32)  117 us
    pallas_call x2, Pallas kernels, attn_call(): pl.pallas_call(functools.partial(kernel, seq, head), grid=(rows // block,...  105 us
    all_gather x4, waiting for transfers between devices, gather(): return lax.all_gather(shard, 'tp', axis=0, tiled=True)  87.5 us
    unnamed x9, local copies, waits for them, and re-layouts  83.6 us
    pallas_call x2, Pallas kernels, rms_rows(): pl.pallas_call(rms_kernel, grid=(rows // ROW_BLOCK,), in_specs=[spec], ou...  82.4 us
  transfers between devices with their start and end apart: 11, of which 7 were waited for; matrix products, arithmetic and copies ran while one was open for 55% of the time, Pallas kernels for 18%

profile of v1, /device:TPU:0, one launch (start us, length us, event | category | flops | bytes accessed | tf_op | source)
XLA Modules:
  0.0 1492.5 jit_solution(15799472739218933699)
XLA Ops:
  7.2 0.0 all-gather.7.cloned.1.call-start
  7.2 0.7 all-gather.7.cloned.1.call-update
  7.9 0.0 reduce-scatter.4.cloned.1.call-start
  8.0 35.3 %rms_rows.2 = bf16[3072,4096]{1,0:T(8,128)(2,1)} custom-call(f32[3072,4096]{1,0:T(8,128)} %bitcast.77), custom_call_target="tpu_custom_call" | custom-call | flops 3221225472 | bytes 75497472 | tf_op jit(solution)/shard_map/rms_rows/pallas_call | solution.py:33
  43.3 68.4 %multiply_convert_fusion = (bf16[3072,2048]{1,0:T(8,128)(2,1)}, f32[3072,2048]{1,0:T(8,128)}) fusion(bf16[3072,4096]{1,0:T(8,128)(2,1)} %rms_rows.2, bf16[1,4096,2048]{2,1,0:T(8,128)(2,1)} %param.14), kind=kOutput, calls=%fused_computation.12 | convolution fusion | flops 51596230656 | bytes 79691776 | tf_op jit(solution)/shard_map/dot_general | solution.py:18
  111.6 12.1 constant_dynamic-slice_fusion.5
  123.8 33.9 %fusion.9 = f32[1536,4096]{1,0:T(8,128)} fusion(bf16[1536,2048]{1,0:T(8,128)(2,1)} %bitcast.93, bf16[1,2048,4096]{2,1,0:T(8,128)(2,1)} %param.15), kind=kOutput, calls=%fused_computation.17 | convolution fusion | flops 25769803776 | bytes 48234496 | tf_op jit(solution)/shard_map/dot_general | solution.py:18
  157.6 1.3 collective-permute-start
  158.9 25.7 %bitcast_convert_fusion = bf16[3072,4096]{1,0:T(8,128)(2,1)} fusion(f32[32,96,4096]{2,1,0:T(8,128)} %param.11), kind=kLoop, calls=%fused_computation.37 | loop fusion | flops 12582912 | bytes 75497472 | tf_op jit(solution)/shard_map/convert_element_type | solution.py:153
  184.7 13.6 collective-permute-done
  198.3 35.5 %convolution_add_fusion = f32[1536,4096]{1,0:T(8,128)} fusion(f32[1536,4096]{1,0:T(8,128)} %collective-permute-done, bf16[1536,2048]{1,0:T(8,128)(2,1)} %bitcast.91, bf16[1,2048,4096]{2,1,0:T(8,128)(2,1)} %param.15), kind=kOutput, calls=%fused_computation.13 | convolution fusion | flops 25776095232 | bytes 73400320 | tf_op jit(solution)/shard_map/dot_general | solution.py:18
  233.8 0.0 all-gather.7.cloned.1.call-done
  233.8 0.0 reduce-scatter.4.cloned.1.call-update
  233.8 0.0 reduce-scatter.6.cloned.1.call-start
  233.9 74.1 %fusion.6 = bf16[3072,2048]{1,0:T(8,128)(2,1)} fusion(f32[3072,2048]{1,0:T(8,128)} %get-tuple-element.75, bf16[3072,4096]{1,0:T(8,128)(2,1)} %bitcast_convert_fusion, bf16[1,2048,4096]{2,1,0:T(8,128)(2,1)} %param.15), kind=kOutput, calls=%fused_computation.9 | convolution fusion | flops 51665436672 | bytes 79691776 | tf_op jit(solution)/shard_map/dot_general | solution.py:18
  308.0 12.5 constant_dynamic-slice_fusion.3
  320.4 0.0 copy-start
  320.4 33.1 %fusion.18 = bf16[1536,4096]{1,0:T(8,128)(2,1)} fusion(bf16[1536,2048]{1,0:T(8,128)(2,1)} %bitcast.94, bf16[1,4096,2048]{2,1,0:T(8,128)(2,1)} %param.14), kind=kOutput, calls=%fused_computation.26 | convolution fusion | flops 25776095232 | bytes 35651584 | tf_op jit(solution)/shard_map/dot_general | solution.py:18
  353.5 0.8 collective-permute-start.1
  354.3 19.1 %collective-permute-done.1 = bf16[1536,4096]{1,0:T(8,128)(2,1)} collective-permute-done((bf16[1536,4096]{1,0:T(8,128)(2,1)}, bf16[1536,4096]{1,0:T(8,128)(2,1)}, u32[]{:S(2)}, u32[]{:S(2)}) %collective-permute-start.1) | collective-permute-done | bytes 12582944 | tf_op jit(solution)/shard_map/ppermute | solution.py:132
  373.4 0.0 copy-done
  373.4 32.0 %add_convert_fusion.1 = bf16[1536,4096]{1,0:T(8,128)(2,1)} fusion(bf16[1536,4096]{1,0:T(8,128)(2,1)} %collective-permute-done.1, bf16[1536,2048]{1,0:T(8,128)(2,1)S(1)} %bitcast.92, bf16[1,4096,2048]{2,1,0:T(8,128)(2,1)} %param.14), kind=kOutput, calls=%fused_computation.11 | convolution fusion | flops 25788678144 | bytes 48234496 | tf_op jit(solution)/shard_map/dot_general | solution.py:18
  405.5 0.0 reduce-scatter.6.cloned.1.call-update
  405.5 0.0 all-gather.9.cloned.1.call-start
  405.5 47.5 %reduce-scatter.4.cloned.1.call-done = f32[384,4096]{1,0:T(8,128)} async-done(((f32[1536,4096]{1,0:T(8,128)}), f32[384,4096]{1,0:T(8,128)}) %reduce-scatter.4.cloned.1.call-update) | async-done | bytes 6291472 | tf_op jit(solution)/shard_map/reduce_scatter | solution.py:136
  453.0 9.1 dynamic-slice_subtract_fusion
  462.1 0.0 all-gather.9.cloned.1.call-update
  462.1 0.0 all-gather.11.cloned.1.call-start
  462.2 109.5 %reduce-scatter.6.cloned.1.call-done = bf16[384,4096]{1,0:T(8,128)(2,1)} async-done(((bf16[1536,4096]{1,0:T(8,128)(2,1)}), bf16[384,4096]{1,0:T(8,128)(2,1)}) %reduce-scatter.6.cloned.1.call-update) | async-done | bytes 3145744 | tf_op jit(solution)/shard_map/reduce_scatter | solution.py:136
  571.7 0.0 all-gather.11.cloned.1.call-update
  571.8 0.0 all-gather.15.cloned.1.call-start
  571.8 21.0 %copy.18 = bf16[1,4096,4,3,128]{1,4,3,2,0:T(8,128)(2,1)} copy(bf16[1,4096,4,3,128]{4,2,3,1,0:T(4,128)(2,1)} %param.12) | data formatting | bytes 25165824 | tf_op args[4]
  592.8 63.5 %convolution_bitcast_fusion = f32[4096,2048]{0,1:T(8,128)} fusion(bf16[3072,2048]{1,0:T(8,128)(2,1)} %fusion.6, bf16[3072,4096]{1,0:T(8,128)(2,1)} %rms_rows.2), kind=kOutput, calls=%fused_computation.14 | convolution fusion | flops 51539607552 | bytes 71303168 | tf_op jit(solution)/shard_map/dot_general | solution.py:18
  656.3 67.3 %fusion.25 = f32[2048,4096]{1,0:T(8,128)} fusion(bf16[3072,2048]{1,0:T(8,128)(2,1)} %get-tuple-element.74, bf16[3072,4096]{1,0:T(8,128)(2,1)} %bitcast_convert_fusion), kind=kOutput, calls=%fused_computation.38 | convolution fusion | flops 51539607552 | bytes 71303168 | tf_op jit(solution)/shard_map/dot_general | solution.py:18
  723.7 76.9 %all-gather.9.cloned.1.call-done.x_ref = f32[3072,4096]{1,0:T(8,128)} async-done(((f32[384,4096]{1,0:T(8,128)}), f32[3072,4096]{1,0:T(8,128)}) %all-gather.9.cloned.1.call-update) | async-done | bytes 50331664 | tf_op jit(solution)/shard_map/all_gather | solution.py:140
  800.5 47.1 %rms_rows.3 = (bf16[3072,4096]{1,0:T(8,128)(2,1)}, f32[3072,4096]{1,0:T(8,128)}) custom-call(f32[3072,4096]{1,0:T(8,128)} %all-gather.9.cloned.1.call-done.x_ref), custom_call_target="tpu_custom_call" | custom-call | flops 3221225472 | bytes 75497472 | tf_op jit(solution)/shard_map/rms_rows/pallas_call | solution.py:33
  847.7 51.2 %convolution_convert_fusion.1.qkv_ref = bf16[3072,1536]{1,0:T(8,128)(2,1)} fusion(bf16[3072,4096]{1,0:T(8,128)(2,1)} %get-tuple-element.35, bf16[4096,1536]{0,1:T(8,128)(2,1)} %bitcast.87), kind=kOutput, calls=%fused_computation.28 | convolution fusion | flops 38659424256 | bytes 47185920 | tf_op jit(solution)/shard_map/dot_general | solution.py:18
  898.9 43.6 %shard_map.143 = bf16[3072,512]{1,0:T(8,128)(2,1)} custom-call(bf16[3072,1536]{1,0:T(8,128)(2,1)} %convolution_convert_fusion.1.qkv_ref), custom_call_target="tpu_custom_call" | custom-call | flops 19327352832 | bytes 12582912 | tf_op jit(solution)/shard_map/pallas_call | solution.py:105
  942.5 0.0 all-gather.11.cloned.1.call-done.grad_ref
  942.5 0.0 all-gather.15.cloned.1.call-update
  942.5 0.0 reduce-scatter.8.cloned.1.call-start
  942.6 76.0 %rms_back_rows.2 = (f32[3072,4096]{1,0:T(8,128)}, bf16[3072,4096]{1,0:T(8,128)(2,1)}) custom-call(f32[3072,4096]{1,0:T(8,128)} %bitcast.78, bf16[3072,4096]{1,0:T(8,128)(2,1)} %all-gather.11.cloned.1.call-done.grad_ref, f32[3072,4096]{1,0:T(8,128)} %bitcast.81), custom_call_target="tpu_custom_call" | custom-call | flops 6442450944 | bytes 201326592 | tf_op jit(solution)/shard_map/rms_back_rows/pallas_call | solution.py:60
  1018.6 20.5 %convolution_convert_fusion.2.grad_o_ref = bf16[3072,512]{1,0:T(8,128)(2,1)} fusion(bf16[3072,4096]{1,0:T(8,128)(2,1)} %get-tuple-element.37, bf16[512,4096]{1,0:T(8,128)(2,1)} %bitcast.98), kind=kOutput, calls=%fused_computation.30 | convolution fusion | flops 12886474752 | bytes 32505856 | tf_op jit(solution)/shard_map/dot_general | solution.py:18
  1039.1 61.3 %shard_map.144 = bf16[3072,1536]{1,0:T(8,128)(2,1)} custom-call(bf16[3072,1536]{1,0:T(8,128)(2,1)} %convolution_convert_fusion.1.qkv_ref, bf16[3072,512]{1,0:T(8,128)(2,1)} %convolution_convert_fusion.2.grad_o_ref), custom_call_target="tpu_custom_call" | custom-call | flops 19327352832 | bytes 12582912 | tf_op jit(solution)/shard_map/pallas_call | solution.py:105
  1100.4 8.0 constant_dynamic-slice_fusion
  1108.4 0.0 all-gather.15.cloned.1.call-done
  1108.4 0.0 copy-start.2
  1108.4 25.6 %convolution_convert_fusion = bf16[1536,4096]{1,0:T(8,128)(2,1)} fusion(bf16[1536,1536]{1,0:T(8,128)(2,1)} %bitcast.96, bf16[4096,1536]{0,1:T(8,128)(2,1)} %bitcast.88), kind=kOutput, calls=%fused_computation.27 | convolution fusion | flops 19333644288 | bytes 29884416 | tf_op jit(solution)/shard_map/dot_general | solution.py:18
  1134.1 0.0 collective-permute-start.2
  1134.1 0.0 copy-done.2
  1134.1 20.6 %fusion.26 = f32[512,4096]{1,0:T(8,128)} fusion(bf16[3072,512]{1,0:T(8,128)(2,1)S(1)} %copy-done.2, bf16[3072,4096]{1,0:T(8,128)(2,1)} %get-tuple-element.37), kind=kOutput, calls=%fused_computation.39 | convolution fusion | flops 12884901888 | bytes 36700160 | tf_op jit(solution)/shard_map/dot_general | solution.py:18
  1154.7 0.0 collective-permute-done.2
  1154.7 0.0 copy-done.1
  1154.7 27.3 %add_convert_fusion = bf16[1536,4096]{1,0:T(8,128)(2,1)} fusion(bf16[1536,4096]{1,0:T(8,128)(2,1)} %collective-permute-done.2, bf16[1536,1536]{1,0:T(8,128)(2,1)S(1)} %bitcast.95, bf16[4096,1536]{0,1:T(8,128)(2,1)} %bitcast.89), kind=kOutput, calls=%fused_computation.10 | convolution fusion | flops 19346227200 | bytes 42467328 | tf_op jit(solution)/shard_map/dot_general | solution.py:18
  1182.0 0.0 reduce-scatter.8.cloned.1.call-update
  1182.1 0.0 all-gather.13.cloned.1.call-start
  1182.1 116.6 %bitcast_subtract_fusion = f32[3072,4096]{1,0:T(8,128)} fusion(f32[3072,4096]{1,0:T(8,128)} %bitcast.79, bf16[8,3072,512]{2,1,0:T(8,128)(2,1)} %bitcast.103, bf16[8,512,4096]{2,1,0:T(8,128)(2,1)} %bitcast.102), kind=kOutput, calls=%fused_computation | convolution fusion | flops 103091798016 | bytes 159383552 | tf_op jit(solution)/shard_map/jtk,jkd->td/dot_general | solution.py:177
  1298.7 0.2 reduce-scatter.8.cloned.1.call-done
  1298.9 0.0 all-gather.13.cloned.1.call-update
  1298.9 33.9 %copy.20 = f32[1,4096,2048]{2,1,0:T(8,128)} copy(f32[1,4096,2048]{1,2,0:T(8,128)} %bitcast.83) | data formatting | bytes 67108864
  1332.8 48.4 %fusion.27 = f32[4096,1536]{0,1:T(8,128)} fusion(bf16[3072,4096]{1,0:T(8,128)(2,1)} %get-tuple-element.35, bf16[3072,1536]{1,0:T(8,128)(2,1)} %shard_map.144), kind=kOutput, calls=%fused_computation.40 | convolution fusion | flops 38654705664 | bytes 59768832 | tf_op jit(solution)/shard_map/dot_general | solution.py:18
  1381.1 28.7 %copy.19 = f32[1,4096,4,3,128]{4,2,3,1,0:T(4,128)} copy(f32[1,4096,4,3,128]{1,4,3,2,0:T(8,128)} %bitcast.84) | data formatting | bytes 50331648
  1409.8 10.6 all-gather.13.cloned.1.call-done.grad_ref
  1420.4 64.8 %rms_back_rows.3 = f32[3072,4096]{1,0:T(8,128)} custom-call(f32[3072,4096]{1,0:T(8,128)} %all-gather.9.cloned.1.call-done.x_ref, bf16[3072,4096]{1,0:T(8,128)(2,1)} %all-gather.13.cloned.1.call-done.grad_ref, f32[3072,4096]{1,0:T(8,128)} %bitcast.80), custom_call_target="tpu_custom_call" | custom-call | flops 6442450944 | bytes 201326592 | tf_op jit(solution)/shard_map/rms_back_rows/pallas_call | solution.py:60
  (1 shorter events, 0.0 us)
Async XLA Ops:
  7.2 226.6 %all-gather.7.cloned.1.call-start = ((), (), s32[]{:S(2)}) async-start(), calls=%async_computation.3 | async-start | bytes 37748736 | tf_op jit(solution)/shard_map/all_gather | solution.py:140
  7.9 445.1 %reduce-scatter.4.cloned.1.call-start = ((), (), s32[]{:S(2)}) async-start(), calls=%async_computation.4 | async-start | bytes 31457280 | tf_op jit(solution)/shard_map/reduce_scatter | solution.py:136
  157.6 40.7 %collective-permute-start = (f32[1536,4096]{1,0:T(8,128)}, f32[1536,4096]{1,0:T(8,128)}, u32[]{:S(2)}, u32[]{:S(2)}) collective-permute-start(f32[1536,4096]{1,0:T(8,128)} %fusion.9), channel_id=1, source_target_pairs={{0,1},{1,0},{2,3},{3,2},{4,5},{5,4},{6,7},{7,6}} | collective-permute-start | bytes 75497480 | tf_op jit(solution)/shard_map/ppermute | solution.py:132
  233.8 337.9 %reduce-scatter.6.cloned.1.call-start = ((), (), s32[]{:S(2)}) async-start(), calls=%async_computation.6 | async-start | bytes 15728640 | tf_op jit(solution)/shard_map/reduce_scatter | solution.py:136
  320.4 53.0 %copy-start = (bf16[4,1,384,2048]{3,2,1,0:T(8,128)(2,1)S(1)}, bf16[4,1,384,2048]{3,2,1,0:T(8,128)(2,1)}, u32[]{:S(2)}) copy-start(bf16[4,1,384,2048]{3,2,1,0:T(8,128)(2,1)} %get-tuple-element.68) | copy-start | bytes 18874372
  353.5 19.9 %collective-permute-start.1 = (bf16[1536,4096]{1,0:T(8,128)(2,1)}, bf16[1536,4096]{1,0:T(8,128)(2,1)}, u32[]{:S(2)}, u32[]{:S(2)}) collective-permute-start(bf16[1536,4096]{1,0:T(8,128)(2,1)} %fusion.18), channel_id=1, source_target_pairs={{0,1},{1,0},{2,3},{3,2},{4,5},{5,4},{6,7},{7,6}} | collective-permute-start | bytes 37748744 | tf_op jit(solution)/shard_map/ppermute | solution.py:132
  405.5 395.1 %all-gather.9.cloned.1.call-start = ((), (), s32[]{:S(2)}) async-start(), calls=%async_computation.5 | async-start | bytes 56623104 | tf_op jit(solution)/shard_map/all_gather | solution.py:140
  462.1 480.3 %all-gather.11.cloned.1.call-start = ((), (), s32[]{:S(2)}) async-start(), calls=%async_computation.7 | async-start | bytes 28311552 | tf_op jit(solution)/shard_map/all_gather | solution.py:140
  571.8 536.7 %all-gather.15.cloned.1.call-start = ((), (), s32[]{:S(2)}) async-start(), calls=%async_computation.10 | async-start | bytes 28311552 | tf_op jit(solution)/shard_map/all_gather | solution.py:171
  942.5 356.4 %reduce-scatter.8.cloned.1.call-start = ((), (), s32[]{:S(2)}) async-start(), calls=%async_computation.8 | async-start | bytes 15728640 | tf_op jit(solution)/shard_map/reduce_scatter | solution.py:136
  1108.4 25.6 %copy-start.2 = (bf16[3072,512]{1,0:T(8,128)(2,1)S(1)}, bf16[3072,512]{1,0:T(8,128)(2,1)}, u32[]{:S(2)}) copy-start(bf16[3072,512]{1,0:T(8,128)(2,1)} %shard_map.143) | copy-start | bytes 9437188
  1134.1 20.6 %copy-start.1 = (bf16[4,1,384,1536]{3,2,1,0:T(8,128)(2,1)S(1)}, bf16[4,1,384,1536]{3,2,1,0:T(8,128)(2,1)}, u32[]{:S(2)}) copy-start(bf16[4,1,384,1536]{3,2,1,0:T(8,128)(2,1)} %get-tuple-element.73) | copy-start | bytes 14155780
  1134.1 20.6 %collective-permute-start.2 = (bf16[1536,4096]{1,0:T(8,128)(2,1)}, bf16[1536,4096]{1,0:T(8,128)(2,1)}, u32[]{:S(2)}, u32[]{:S(2)}) collective-permute-start(bf16[1536,4096]{1,0:T(8,128)(2,1)} %convolution_convert_fusion), channel_id=1, source_target_pairs={{0,1},{1,0},{2,3},{3,2},{4,5},{5,4},{6,7},{7,6}} | collective-permute-start | bytes 37748744 | tf_op jit(solution)/shard_map/ppermute | solution.py:132
  1182.1 238.3 %all-gather.13.cloned.1.call-start = ((), (), s32[]{:S(2)}) async-start(), calls=%async_computation.9 | async-start | bytes 28311552 | tf_op jit(solution)/shard_map/all_gather | solution.py:140
Sparse Core Ops, SparseCore 0:
  9.8 160.1 all-gather.6
  233.9 219.0 reduce-scatter.3
  456.6 115.0 reduce-scatter.5
  574.0 226.4 all-gather.8
  802.2 119.6 all-gather.10
  942.6 119.3 all-gather.14
  1182.2 116.6 reduce-scatter.7
  1300.7 119.6 all-gather.12

commit v2 on v1

v2 whole, which is shorter than its diff:
```python
import functools
import math
import jax
import jax.numpy as jnp
from jax import lax
from jax.experimental import pallas as pl
from jax.experimental.layout import Layout, with_layout_constraint
from jax.sharding import PartitionSpec as P


NORM_EPS = 1e-6
ROW_BLOCK = 128
SEQ_BLOCK = 2
PARTS = 2
F32 = jnp.float32
BF16 = jnp.bfloat16


def dot(lhs, rhs, lhs_dim, rhs_dim):
    return lax.dot_general(lhs, rhs, (((lhs_dim,), (rhs_dim,)), ((), ())), preferred_element_type=F32)


def row_call(kernel, rows, base, arrays, outs, flops, carried=()):
    width = arrays[0].shape[1]
    first = base // ROW_BLOCK
    spec = lambda tall: pl.BlockSpec((ROW_BLOCK, width), lambda i: (i + first if tall else i, 0))
    n_in, n_out = len(arrays), len(outs)

    def body(*refs):
        kernel(*refs[:n_in], *refs[n_in + len(carried):])

    return pl.pallas_call(
        body,
        grid=(rows // ROW_BLOCK,),
        in_specs=[spec(array.shape[0] > rows) for array in arrays] + [pl.BlockSpec(memory_space=pl.ANY)] * len(carried),
        out_specs=[spec(out.shape[0] > rows) for out in outs],
        out_shape=outs,
        input_output_aliases={n_in + i: n_out - len(carried) + i for i in range(len(carried))},
        cost_estimate=pl.CostEstimate(flops=rows * width * flops, bytes_accessed=rows * width * 12, transcendentals=0),
    )(*arrays, *carried)


def rms_kernel(x_ref, n_ref, *copy_ref):
    x_in = x_ref[...]
    inv_rms = lax.rsqrt(jnp.mean(x_in * x_in, axis=-1, keepdims=True) + NORM_EPS)
    n_ref[...] = (x_in * inv_rms).astype(BF16)
    for ref in copy_ref:
        ref[...] = x_in


def rms_back_kernel(x_ref, grad_ref, cot_ref, *out_refs):
    x_in = x_ref[...]
    grad_n = grad_ref[...].astype(F32)
    inv_rms = lax.rsqrt(jnp.mean(x_in * x_in, axis=-1, keepdims=True) + NORM_EPS)
    normed = x_in * inv_rms
    inner = jnp.mean(normed * grad_n, axis=-1, keepdims=True)
    total = cot_ref[...] + inv_rms * (grad_n - normed * inner)
    for ref in out_refs:
        ref[...] = total.astype(ref.dtype)


def head_probs(qkv_ref, rows, col, head):
    q_rows, k_rows, v_rows = (qkv_ref[rows, pl.ds(col + part * head, head)] for part in range(3))
    scores = dot(q_rows, k_rows, 1, 1) * (1.0 / math.sqrt(head))
    unnorm = jnp.exp(scores - jnp.max(scores, axis=-1, keepdims=True))
    return q_rows, k_rows, v_rows, unnorm / jnp.sum(unnorm, axis=-1, keepdims=True)


def attn_kernel(seq, head, qkv_ref, grad_o_ref, out_ref, grad_ref):
    for start in range(0, qkv_ref.shape[0], seq):
        rows = pl.ds(start, seq)
        for idx in range(grad_o_ref.shape[1] // head):
            col = 3 * head * idx
            mine = pl.ds(idx * head, head)
            q_rows, k_rows, v_rows, prob = head_probs(qkv_ref, rows, col, head)
            prob_bf = prob.astype(BF16)
            out_ref[rows, mine] = dot(prob_bf, v_rows, 1, 0).astype(BF16)
            grad_o = grad_o_ref[rows, mine]
            grad_p = dot(grad_o, v_rows, 1, 1)
            inner = jnp.sum(grad_p * prob, axis=-1, keepdims=True)
            grad_s = (prob * (grad_p - inner) * (1.0 / math.sqrt(head))).astype(BF16)
            grads = (dot(grad_s, k_rows, 1, 0), dot(grad_s, q_rows, 0, 0), dot(prob_bf, grad_o, 0, 0))
            for part, grad in enumerate(grads):
                grad_ref[rows, pl.ds(col + part * head, head)] = grad.astype(BF16)


def attn_call(seq, head, base, qkv, grad_o):
    rows, cols = qkv.shape
    block = SEQ_BLOCK * seq
    spec = lambda width, first: pl.BlockSpec((block, width), lambda i: (i + first, 0))
    return pl.pallas_call(
        functools.partial(attn_kernel, seq, head),
        grid=(rows // block,),
        in_specs=[spec(cols, 0), spec(grad_o.shape[1], base // block)],
        out_specs=[spec(grad_o.shape[1], 0), spec(cols, 0)],
        out_shape=[jax.ShapeDtypeStruct((rows, grad_o.shape[1]), BF16), jax.ShapeDtypeStruct((rows, cols), BF16)],
        cost_estimate=pl.CostEstimate(flops=rows * 3072 * 4096, bytes_accessed=rows * 8192, transcendentals=0),
        name="attn",
    )(qkv, grad_o)


def solution(mesh):
    n_tp = mesh.shape["tp"]
    act_spec = P("dp", None, None)
    weight_specs = (P(None, None, "tp", None, None), P(None, "tp", None, None), P(None, None, "tp"), P(None, "tp", None))
    grad_specs = (P("dp", None, "tp", None, None), P("dp", "tp", None, None), P("dp", None, "tp"), P("dp", "tp", None))
    partner = [(i, i ^ 1) for i in range(n_tp)]
    chips = [[i for i in range(n_tp) if i % 2 == core] for core in range(2)]

    def halves(rows_in, parts):
        core = lax.rem(lax.axis_index("tp"), 2)
        blocks = rows_in.reshape(parts, n_tp // 2, 2, -1, rows_in.shape[1])
        pick = lambda which: lax.dynamic_index_in_dim(blocks, which, 2, keepdims=False).swapaxes(0, 1)
        return tuple(pick(which).reshape(-1, rows_in.shape[1]) for which in (core, 1 - core))

    def scatter_product(lhs, rhs, rhs_dim, travel, parts=1, fill=(), behind=(), after=()):
        keep, send = halves(lhs, parts)
        send, after = lax.optimization_barrier((send, after))
        got = lax.ppermute(dot(send, rhs, 1, rhs_dim).astype(travel), "tp", partner)
        keep, fill = lax.optimization_barrier((keep, fill))
        chip_sum = (dot(keep, rhs, 1, rhs_dim) + got.astype(F32)).astype(travel)
        chip_sum, fill, behind = lax.optimization_barrier((chip_sum, fill, behind))
        own = lax.psum_scatter(chip_sum, "tp", scatter_dimension=0, tiled=True, axis_index_groups=chips)
        return own, fill, behind, after

    def gather(shard):
        return lax.all_gather(shard, "tp", axis=0, tiled=True)

    def layer(run_y1, run_y2, run_c1, run_c2, w_qkv, w_out, w_up, w_down, seqs):
        rows, width = run_y1.shape
        seq = rows // seqs
        heads, head = w_qkv.shape[1], w_qkv.shape[3]
        part_rows = rows // PARTS
        share = part_rows // n_tp
        full = lambda dtype: jax.ShapeDtypeStruct((rows, width), dtype)
        wq_mat = w_qkv.reshape(width, heads * 3 * head)
        wo_mat = w_out.reshape(heads * head, width)
        wo_all = gather(wo_mat).reshape(n_tp, heads * head, width)

        (n1,) = row_call(rms_kernel, rows, 0, (run_y1,), (full(BF16),), 256)
        hidden = dot(n1, w_up, 1, 0)
        act_f, gelu_back = jax.vjp(jax.nn.gelu, hidden)
        act_bf = act_f.astype(BF16)
        c2_bf = run_c2.astype(BF16)
        g_own, c2_bf, wo_all, _ = scatter_product(act_bf, w_down, 0, F32, PARTS, c2_bf, wo_all)
        y2_own = lax.dynamic_index_in_dim(run_y2.reshape(PARTS, n_tp, share, width), lax.axis_index("tp"), 1, keepdims=False)

        grad_hid = gelu_back(dot(c2_bf, w_down, 1, 1))[0].astype(BF16)
        gn_own = scatter_product(grad_hid, w_up, 1, BF16)[0]
        gn = gather(gn_own)
        x2 = [gather(y2_own[part] - g_own[part * share:(part + 1) * share]) for part in range(PARTS)]
        g_down = dot(act_bf, c2_bf, 0, 0)
        g_up = with_layout_constraint(dot(n1, grad_hid, 0, 0), Layout((0, 1)))
        gn, g_down, g_up = lax.optimization_barrier((gn, g_down, g_up))

        c1, c1_bf = row_call(rms_back_kernel, rows, 0, (run_y1, gn, run_c1), (full(F32), full(BF16)), 512)
        grad_o = dot(c1_bf, wo_mat, 1, 1).astype(BF16)

        outs, g_qkv, fn_own, x2_out, done = [], 0, [], (), ()
        for part in range(PARTS):
            base = part * part_rows
            part_bf = jax.ShapeDtypeStruct((part_rows, width), BF16)
            n2, copy = row_call(rms_kernel, part_rows, base, (x2[part],), (part_bf, full(F32)), 256, x2_out)
            x2_out = (copy,)
            qkv = dot(n2, wq_mat, 1, 0).astype(BF16)
            qkv, fn_own = lax.optimization_barrier((qkv, fn_own))
            attn_out, grad_qkv = attn_call(seq, head, base, qkv, grad_o)
            outs.append(attn_out)
            g_qkv = g_qkv + dot(n2, grad_qkv, 0, 0)
            if part == PARTS - 1:
                all_out = jnp.concatenate(outs)
                o_all = lax.all_gather(all_out, "tp", axis=0)
                g_out = dot(all_out, c1_bf, 0, 0).reshape(w_out.shape)
                done = (g_out, with_layout_constraint(g_qkv.reshape(w_qkv.shape), Layout((0, 2, 1, 3))))
            own, done, later, _ = scatter_product(grad_qkv, wq_mat, 1, BF16, 1, done, x2[part + 1:])
            x2[part + 1:] = later
            fn_own.append(own)
        x1 = run_y1 - jnp.einsum("jtk,jkd->td", o_all, wo_all, preferred_element_type=F32)
        fn_own[-1], x1 = lax.optimization_barrier((fn_own[-1], x1))
        fn = [gather(own) for own in fn_own]
        g_out, g_qkv = done
        c2 = ()
        for part in range(PARTS):
            c2 = row_call(rms_back_kernel, part_rows, part * part_rows, (x2[part], fn[part], run_c2), (full(F32),), 512, c2)
        return x1, x2_out[0], c1, c2[0], g_qkv, g_out, g_up, g_down

    def local_backward(out_y1, out_y2, cot_y1, cot_y2, w_qkv, w_out, w_up, w_down):
        seqs, width = out_y1.shape[0], out_y1.shape[2]
        state = tuple(array.reshape(-1, width) for array in (out_y1, out_y2, cot_y1, cot_y2))
        per_layer = []
        for idx in reversed(range(w_qkv.shape[0])):
            result = layer(*state, w_qkv[idx], w_out[idx], w_up[idx], w_down[idx], seqs)
            state = result[:4]
            per_layer.insert(0, result[4:])
        stacked = tuple(jnp.stack(slot) for slot in zip(*per_layer))
        return tuple(array.reshape(out_y1.shape) for array in state) + stacked

    return jax.shard_map(local_backward, mesh=mesh, in_specs=(act_spec,) * 4 + weight_specs, out_specs=(act_spec,) * 4 + grad_specs, check_vma=False)
```

time: 1500 us -> 1640 us (1.093)
  waiting for transfers between devices: 278 us -> 442 us
  local copies, waits for them, and re-layouts: 116 us -> 92 us
  matrix products: 718 us -> 737 us
  Pallas kernels: 328 us -> 311 us
    reduce_scatter x3 -> x4, waiting for transfers between devices: 157 us -> 348 us  [scatter_product(): lax.psum_scatter(chip_sum, 'tp', scatter_dimension=0, tiled=True, axis_in...]
    unnamed x9 -> x30, local copies, waits for them, and re-layouts: 83.6 us -> 23.4 us
    all_gather x4 -> x6, waiting for transfers between devices: 87.5 us -> 51.6 us  [gather(): return lax.all_gather(shard, 'tp', axis=0, tiled=True)]
    reshape x0 -> x1, local copies, waits for them, and re-layouts: none -> 28.8 us  [layer(): g_qkv.reshape(w_qkv.shape)]
    dot_general x14 -> x18, matrix products: 601 us -> 621 us  [dot(): lax.dot_general(lhs, rhs, (((lhs_dim,), (rhs_dim,)), ((), ())), preferred...]
    pallas_call x6 -> x8, Pallas kernels: 328 us -> 311 us  [the longest x6 227 us: row_call(): pl.pallas_call(body, grid=(rows // ROW_BLOCK,), in_specs=[spec(array.shap...]
    ppermute x3 -> x4, waiting for transfers between devices: 32.8 us -> 39.7 us  [scatter_product(): got = lax.ppermute(dot(send, rhs, 1, rhs_dim).astype(travel), 'tp', partner)]
    dynamic_slice x3 -> x6, local copies, waits for them, and re-layouts: 32.6 us -> 38.3 us  [halves(): lax.dynamic_index_in_dim(blocks, which, 2, keepdims=False).swapaxes(0, 1)]
  transfers between devices with their start and end apart: 11 -> 15, of which waited for: 7 -> 8; matrix products, arithmetic and copies ran while one was open for 55% -> 43% of each run, Pallas kernels for 18% -> 14%
where the time goes in v2:
time: 1640 us; the launch traced here: 1630 us
  matrix products  737 us (45%)
  waiting for transfers between devices  442 us (27%)
  Pallas kernels  311 us (19%)
  local copies, waits for them, and re-layouts  92 us (6%)
  other arithmetic  35.4 us (2%)
    dot_general x18, matrix products, dot(): lax.dot_general(lhs, rhs, (((lhs_dim,), (rhs_dim,)), ((), ())), preferred...  621 us
    reduce_scatter x4, waiting for transfers between devices, scatter_product(): lax.psum_scatter(chip_sum, 'tp', scatter_dimension=0, tiled=True, axis_in...  348 us
    pallas_call x6, Pallas kernels, row_call(): pl.pallas_call(body, grid=(rows // ROW_BLOCK,), in_specs=[spec(array.shap...  227 us
    dot_general x1, matrix products, layer(): jnp.einsum('jtk,jkd->td', o_all, wo_all, preferred_element_type=F32)  116 us
    pallas_call x2, Pallas kernels, attn_call(): pl.pallas_call(functools.partial(attn_kernel, seq, head), grid=(rows // b...  84.1 us
    all_gather x6, waiting for transfers between devices, gather(): return lax.all_gather(shard, 'tp', axis=0, tiled=True)  51.6 us
    ppermute x4, waiting for transfers between devices, scatter_product(): got = lax.ppermute(dot(send, rhs, 1, rhs_dim).astype(travel), 'tp', partner)  39.7 us
    dynamic_slice x6, local copies, waits for them, and re-layouts, halves(): lax.dynamic_index_in_dim(blocks, which, 2, keepdims=False).swapaxes(0, 1)  38.3 us
  transfers between devices with their start and end apart: 15, of which 8 were waited for; matrix products, arithmetic and copies ran while one was open for 43% of the time, Pallas kernels for 14%

profile of v2, /device:TPU:0, one launch (start us, length us, event | category | flops | bytes accessed | tf_op | source)
XLA Modules:
  0.0 1633.7 jit_solution(3708724197066900081)
XLA Ops:
  7.2 0.0 all-gather.9.cloned.1.call-start
  7.2 0.7 all-gather.9.cloned.1.call-update
  7.9 0.0 reduce-scatter.7.cloned.1.call-start
  8.0 35.3 %shard_map.143 = bf16[3072,4096]{1,0:T(8,128)(2,1)} custom-call(f32[3072,4096]{1,0:T(8,128)} %bitcast.107), custom_call_target="tpu_custom_call" | custom-call | flops 3221225472 | bytes 150994944 | tf_op jit(solution)/shard_map/pallas_call | solution.py:32
  43.3 68.4 %multiply_convert_fusion = (bf16[3072,2048]{1,0:T(8,128)(2,1)}, f32[3072,2048]{1,0:T(8,128)}) fusion(bf16[3072,4096]{1,0:T(8,128)(2,1)} %shard_map.143, bf16[1,4096,2048]{2,1,0:T(8,128)(2,1)} %param.14), kind=kOutput, calls=%fused_computation.11 | convolution fusion | flops 51596230656 | bytes 79691776 | tf_op jit(solution)/shard_map/dot_general | solution.py:20
  111.7 12.1 constant_dynamic-slice_fusion.7
  123.8 3.5 copy.19
  127.4 32.9 %fusion.9 = f32[1536,4096]{1,0:T(8,128)} fusion(bf16[1536,2048]{1,0:T(8,128)(2,1)S(1)} %bitcast.128, bf16[1,2048,4096]{2,1,0:T(8,128)(2,1)} %param.15), kind=kOutput, calls=%fused_computation.17 | convolution fusion | flops 25769803776 | bytes 48234496 | tf_op jit(solution)/shard_map/dot_general | solution.py:20
  160.2 1.3 collective-permute-start
  161.5 3.3 copy.18
  164.8 26.0 %bitcast_convert_fusion = bf16[3072,4096]{1,0:T(8,128)(2,1)} fusion(f32[32,96,4096]{2,1,0:T(8,128)} %param.11), kind=kLoop, calls=%fused_computation.48 | loop fusion | flops 12582912 | bytes 75497472 | tf_op jit(solution)/shard_map/convert_element_type | solution.py:144
  190.8 10.1 collective-permute-done
  200.9 35.5 %convolution_add_fusion = f32[1536,4096]{1,0:T(8,128)} fusion(f32[1536,4096]{1,0:T(8,128)} %collective-permute-done, bf16[1536,2048]{1,0:T(8,128)(2,1)} %bitcast.127, bf16[1,2048,4096]{2,1,0:T(8,128)(2,1)} %param.15), kind=kOutput, calls=%fused_computation.12 | convolution fusion | flops 25776095232 | bytes 73400320 | tf_op jit(solution)/shard_map/dot_general | solution.py:20
  236.4 73.9 %fusion.6 = bf16[3072,2048]{1,0:T(8,128)(2,1)} fusion(f32[3072,2048]{1,0:T(8,128)} %get-tuple-element.79, bf16[3072,4096]{1,0:T(8,128)(2,1)} %bitcast_convert_fusion, bf16[1,2048,4096]{2,1,0:T(8,128)(2,1)} %param.15), kind=kOutput, calls=%fused_computation.9 | convolution fusion | flops 51665436672 | bytes 79691776 | tf_op jit(solution)/shard_map/dot_general | solution.py:20
  310.2 12.1 constant_dynamic-slice_fusion.5
  322.3 33.1 %fusion.18 = bf16[1536,4096]{1,0:T(8,128)(2,1)} fusion(bf16[1536,2048]{1,0:T(8,128)(2,1)} %bitcast.130, bf16[1,4096,2048]{2,1,0:T(8,128)(2,1)} %param.14), kind=kOutput, calls=%fused_computation.26 | convolution fusion | flops 25776095232 | bytes 35651584 | tf_op jit(solution)/shard_map/dot_general | solution.py:20
  355.4 0.4 collective-permute-start.1
  355.8 19.1 %collective-permute-done.1 = bf16[1536,4096]{1,0:T(8,128)(2,1)} collective-permute-done((bf16[1536,4096]{1,0:T(8,128)(2,1)}, bf16[1536,4096]{1,0:T(8,128)(2,1)}, u32[]{:S(2)}, u32[]{:S(2)}) %collective-permute-start.1) | collective-permute-done | bytes 12582944 | tf_op jit(solution)/shard_map/ppermute | solution.py:119
  374.9 31.9 %add_convert_fusion = bf16[1536,4096]{1,0:T(8,128)(2,1)} fusion(bf16[1536,4096]{1,0:T(8,128)(2,1)} %collective-permute-done.1, bf16[1536,2048]{1,0:T(8,128)(2,1)S(1)} %bitcast.129, bf16[1,4096,2048]{2,1,0:T(8,128)(2,1)} %param.14), kind=kOutput, calls=%fused_computation.10 | convolution fusion | flops 25788678144 | bytes 48234496 | tf_op jit(solution)/shard_map/dot_general | solution.py:20
  406.8 0.0 reduce-scatter.5.cloned.1.call-start
  406.9 0.7 reduce-scatter.5.cloned.1.call-update
  407.6 0.0 all-gather.13.cloned.1.call-start
  407.6 117.1 %reduce-scatter.7.cloned.1.call-done = bf16[384,4096]{1,0:T(8,128)(2,1)} async-done(((bf16[1536,4096]{1,0:T(8,128)(2,1)}), bf16[384,4096]{1,0:T(8,128)(2,1)}) %reduce-scatter.7.cloned.1.call-update) | async-done | bytes 3145744 | tf_op jit(solution)/shard_map/reduce_scatter | solution.py:123
  524.7 0.0 all-gather.11.cloned.1.call-start
  524.8 219.7 %reduce-scatter.5.cloned.1.call-done = f32[384,4096]{1,0:T(8,128)} async-done(((f32[1536,4096]{1,0:T(8,128)}), f32[384,4096]{1,0:T(8,128)}) %reduce-scatter.5.cloned.1.call-update) | async-done | bytes 6291472 | tf_op jit(solution)/shard_map/reduce_scatter | solution.py:123
  744.5 9.4 slice_subtract_fusion
  753.9 0.0 all-gather.15.cloned.1.call-start
  754.0 20.2 %copy.20 = bf16[1,4096,4,3,128]{1,4,3,2,0:T(8,128)(2,1)} copy(bf16[1,4096,4,3,128]{4,2,3,1,0:T(4,128)(2,1)} %param.12) | data formatting | bytes 25165824 | tf_op args[4]
  774.2 0.0 reduce-scatter.9.cloned.1.call-start
  774.2 63.5 %convolution_bitcast_fusion = f32[4096,2048]{1,0:T(8,128)} fusion(bf16[3072,2048]{1,0:T(8,128)(2,1)} %fusion.6, bf16[3072,4096]{1,0:T(8,128)(2,1)} %shard_map.143), kind=kOutput, calls=%fused_computation.14 | convolution fusion | flops 51539607552 | bytes 71303168 | tf_op jit(solution)/shard_map/dot_general | solution.py:20
  837.7 63.4 %fusion.25 = f32[2048,4096]{1,0:T(8,128)} fusion(bf16[3072,2048]{1,0:T(8,128)(2,1)} %get-tuple-element.78, bf16[3072,4096]{1,0:T(8,128)(2,1)} %bitcast_convert_fusion), kind=kOutput, calls=%fused_computation.49 | convolution fusion | flops 51539607552 | bytes 71303168 | tf_op jit(solution)/shard_map/dot_general | solution.py:20
  901.2 76.2 %shard_map.145 = (f32[3072,4096]{1,0:T(8,128)}, bf16[3072,4096]{1,0:T(8,128)(2,1)}) custom-call(f32[3072,4096]{1,0:T(8,128)} %bitcast.108, bf16[3072,4096]{1,0:T(8,128)(2,1)} %all-gather.13.cloned.1.call-done.refs_1_, f32[3072,4096]{1,0:T(8,128)} %bitcast.112), custom_call_target="tpu_custom_call" | custom-call | flops 6442450944 | bytes 150994944 | tf_op jit(solution)/shard_map/pallas_call | solution.py:32
  977.4 20.5 %convolution_convert_fusion.4.grad_o_ref = bf16[3072,512]{1,0:T(8,128)(2,1)} fusion(bf16[3072,4096]{1,0:T(8,128)(2,1)} %get-tuple-element.44, bf16[512,4096]{1,0:T(8,128)(2,1)} %bitcast.136), kind=kOutput, calls=%fused_computation.33 | convolution fusion | flops 12886474752 | bytes 32505856 | tf_op jit(solution)/shard_map/dot_general | solution.py:20
  997.8 24.0 %shard_map.144 = (bf16[1536,4096]{1,0:T(8,128)(2,1)}, f32[3072,4096]{1,0:T(8,128)}) custom-call(f32[1536,4096]{1,0:T(8,128)} %all-gather.11.cloned.1.call-done.refs_0_), custom_call_target="tpu_custom_call" | custom-call | flops 1610612736 | bytes 75497472 | tf_op jit(solution)/shard_map/pallas_call | solution.py:32
  1021.9 27.2 %convolution_convert_fusion.1.qkv_ref = bf16[1536,1536]{1,0:T(8,128)(2,1)} fusion(bf16[1536,4096]{1,0:T(8,128)(2,1)} %get-tuple-element.41, bf16[4096,1536]{0,1:T(8,128)(2,1)} %bitcast.117), kind=kOutput, calls=%fused_computation.30 | convolution fusion | flops 19329712128 | bytes 29884416 | tf_op jit(solution)/shard_map/dot_general | solution.py:20
  1049.1 42.0 %attn.2 = (bf16[1536,512]{1,0:T(8,128)(2,1)}, bf16[1536,1536]{1,0:T(8,128)(2,1)}) custom-call(bf16[1536,1536]{1,0:T(8,128)(2,1)} %convolution_convert_fusion.1.qkv_ref, bf16[3072,512]{1,0:T(8,128)(2,1)} %convolution_convert_fusion.4.grad_o_ref), custom_call_target="tpu_custom_call" | custom-call | flops 19327352832 | bytes 12582912 | tf_op jit(solution)/shard_map/attn/pallas_call | solution.py:91
  1091.1 3.0 constant_dynamic-slice_fusion.2
  1094.1 14.7 convolution_convert_fusion.3
  1108.8 10.5 collective-permute-done.2
  1119.3 13.1 add_convert_fusion.2
  1132.4 0.0 all-gather.21.cloned.1.call-start
  1132.4 1.5 constant_dynamic-update-slice_fusion.1
  1133.9 24.3 %shard_map.146 = (bf16[1536,4096]{1,0:T(8,128)(2,1)}, f32[3072,4096]{1,0:T(8,128)}) custom-call(f32[1536,4096]{1,0:T(8,128)} %all-gather.15.cloned.1.call-done.refs_0_, f32[3072,4096]{1,0:T(8,128)} %get-tuple-element.47.refs_1_), custom_call_target="tpu_custom_call", output_to_operand_aliasing={{1}: (1, {})} | custom-call | flops 1610612736 | bytes 75497472 | tf_op jit(solution)/shard_map/pallas_call | solution.py:32
  1158.3 27.0 %convolution_convert_fusion.qkv_ref = bf16[1536,1536]{1,0:T(8,128)(2,1)} fusion(bf16[1536,4096]{1,0:T(8,128)(2,1)} %get-tuple-element.48, bf16[4096,1536]{0,1:T(8,128)(2,1)} %bitcast.119), kind=kOutput, calls=%fused_computation.29 | convolution fusion | flops 19329712128 | bytes 29884416 | tf_op jit(solution)/shard_map/dot_general | solution.py:20
  1185.3 11.5 reduce-scatter.9.cloned.1.call-done
  1196.8 42.1 %attn.3 = (bf16[1536,512]{1,0:T(8,128)(2,1)}, bf16[1536,1536]{1,0:T(8,128)(2,1)}) custom-call(bf16[1536,1536]{1,0:T(8,128)(2,1)} %convolution_convert_fusion.qkv_ref, bf16[3072,512]{1,0:T(8,128)(2,1)} %convolution_convert_fusion.4.grad_o_ref), custom_call_target="tpu_custom_call" | custom-call | flops 19327352832 | bytes 12582912 | tf_op jit(solution)/shard_map/attn/pallas_call | solution.py:91
  1238.8 1.5 constant_dynamic-update-slice_fusion
  1240.4 1.6 copy-done
  1242.0 0.0 reduce-scatter.11.cloned.1.call-start
  1242.1 4.3 constant_dynamic-slice_fusion
  1246.4 17.0 %convolution_convert_fusion.2 = bf16[768,4096]{1,0:T(8,128)(2,1)} fusion(bf16[768,1536]{1,0:T(8,128)(2,1)S(1)} %bitcast.139, bf16[4096,1536]{0,1:T(8,128)(2,1)} %bitcast.120), kind=kOutput, calls=%fused_computation.31 | convolution fusion | flops 9666822144 | bytes 21233664 | tf_op jit(solution)/shard_map/dot_general | solution.py:20
  1263.5 25.8 %fusion.27 = f32[4096,1536]{0,1:T(8,128)} fusion(bf16[1536,4096]{1,0:T(8,128)(2,1)S(1)} %bitcast.146, bf16[1536,1536]{1,0:T(8,128)(2,1)S(1)} %bitcast.133), kind=kOutput, calls=%fused_computation.51 | convolution fusion | flops 19327352832 | bytes 42467328 | tf_op jit(solution)/shard_map/dot_general | solution.py:20
  1289.2 35.0 %convolution_add_fusion.1 = f32[4096,1536]{0,1:T(8,128)} fusion(f32[4096,1536]{0,1:T(8,128)} %fusion.27, bf16[1536,4096]{1,0:T(8,128)(2,1)} %get-tuple-element.48, bf16[1536,1536]{1,0:T(8,128)(2,1)} %get-tuple-element.51), kind=kOutput, calls=%fused_computation.13 | convolution fusion | flops 19333644288 | bytes 67633152 | tf_op jit(solution)/shard_map/dot_general | solution.py:20
  1324.2 28.8 %copy.21 = f32[4096,4,3,128]{3,1,2,0:T(4,128)} copy(f32[4096,4,3,128]{0,3,2,1:T(8,128)} %bitcast.114) | data formatting | bytes 50331648 | tf_op jit(solution)/shard_map/reshape | solution.py:174
  1353.1 20.8 %fusion.26 = f32[512,4096]{1,0:T(8,128)} fusion(bf16[3072,512]{1,0:T(8,128)(2,1)S(1)} %copy-done.1, bf16[3072,4096]{1,0:T(8,128)(2,1)} %get-tuple-element.44), kind=kOutput, calls=%fused_computation.50 | convolution fusion | flops 12884901888 | bytes 36700160 | tf_op jit(solution)/shard_map/dot_general | solution.py:20
  1373.9 17.7 %add_convert_fusion.1 = bf16[768,4096]{1,0:T(8,128)(2,1)} fusion(bf16[768,4096]{1,0:T(8,128)(2,1)} %collective-permute-done.3, bf16[768,1536]{1,0:T(8,128)(2,1)S(1)} %bitcast.137, bf16[4096,1536]{0,1:T(8,128)(2,1)} %bitcast.121), kind=kOutput, calls=%fused_computation.27 | convolution fusion | flops 9673113600 | bytes 27525120 | tf_op jit(solution)/shard_map/dot_general | solution.py:20
  1391.6 0.0 all-gather.19.cloned.1.call-start
  1391.6 0.5 all-gather.19.cloned.1.call-update
  1392.2 0.0 all-gather.17.cloned.1.call-start
  1392.3 116.2 %bitcast_subtract_fusion = f32[3072,4096]{1,0:T(8,128)} fusion(f32[3072,4096]{1,0:T(8,128)} %bitcast.109, bf16[8,3072,512]{2,1,0:T(8,128)(2,1)} %bitcast.144, bf16[8,512,4096]{2,1,0:T(8,128)(2,1)} %bitcast.143), kind=kOutput, calls=%fused_computation | convolution fusion | flops 103091798016 | bytes 159383552 | tf_op jit(solution)/shard_map/jtk,jkd->td/dot_general | solution.py:178
  1508.5 17.2 %all-gather.19.cloned.1.call-done.refs_1_ = bf16[1536,4096]{1,0:T(8,128)(2,1)} async-done(((bf16[192,4096]{1,0:T(8,128)(2,1)}), bf16[1536,4096]{1,0:T(8,128)(2,1)}) %all-gather.19.cloned.1.call-update) | async-done | bytes 12582928 | tf_op jit(solution)/shard_map/all_gather | solution.py:127
  1525.7 33.9 %shard_map.147.refs_3_ = f32[3072,4096]{1,0:T(8,128)} custom-call(f32[1536,4096]{1,0:T(8,128)} %all-gather.11.cloned.1.call-done.refs_0_, bf16[1536,4096]{1,0:T(8,128)(2,1)} %all-gather.19.cloned.1.call-done.refs_1_, f32[3072,4096]{1,0:T(8,128)} %bitcast.105), custom_call_target="tpu_custom_call" | custom-call | flops 3221225472 | bytes 75497472 | tf_op jit(solution)/shard_map/pallas_call | solution.py:32
  1559.6 34.3 %all-gather.17.cloned.1.call-done.refs_1_ = bf16[1536,4096]{1,0:T(8,128)(2,1)} async-done(((bf16[192,4096]{1,0:T(8,128)(2,1)}), bf16[1536,4096]{1,0:T(8,128)(2,1)}) %all-gather.17.cloned.1.call-update) | async-done | bytes 12582928 | tf_op jit(solution)/shard_map/all_gather | solution.py:127
  1594.0 33.0 %shard_map.148 = f32[3072,4096]{1,0:T(8,128)} custom-call(f32[1536,4096]{1,0:T(8,128)} %all-gather.15.cloned.1.call-done.refs_0_, bf16[1536,4096]{1,0:T(8,128)(2,1)} %all-gather.17.cloned.1.call-done.refs_1_, f32[3072,4096]{1,0:T(8,128)} %bitcast.106, f32[3072,4096]{1,0:T(8,128)} %shard_map.147.refs_3_), custom_call_target="tpu_custom_call", output_to_operand_aliasing={{}: (3, {})} | custom-call | flops 3221225472 | bytes 75497472 | tf_op jit(solution)/shard_map/pallas_call | solution.py:32
  (48 shorter events, 0.2 us)
Async XLA Ops:
  7.2 229.2 %all-gather.9.cloned.1.call-start = ((), (), s32[]{:S(2)}) async-start(), calls=%async_computation.4 | async-start | bytes 37748736 | tf_op jit(solution)/shard_map/all_gather | solution.py:127
  7.9 516.8 %reduce-scatter.7.cloned.1.call-start = ((), (), s32[]{:S(2)}) async-start(), calls=%async_computation.7 | async-start | bytes 15728640 | tf_op jit(solution)/shard_map/reduce_scatter | solution.py:123
  123.8 37.7 %slice-start = ((s8[6291456]{0:T(1024)(128)(4,1)}), s8[4194304]{0:T(1024)(128)(4,1)S(1)}, s32[]{:S(2)}) async-start(s8[6291456]{0:T(1024)(128)(4,1)} %bitcast.115), calls=%async_computation.15 | async-start | bytes 8388608
  127.4 34.1 %slice-start.1 = ((s8[6291456]{0:T(1024)(128)(4,1)}), s8[2097152]{0:T(1024)(128)(4,1)S(1)}, s32[]{:S(2)}) async-start(s8[6291456]{0:T(1024)(128)(4,1)} %bitcast.115), calls=%async_computation.16 | async-start | bytes 4194304
  160.2 40.6 %collective-permute-start = (f32[1536,4096]{1,0:T(8,128)}, f32[1536,4096]{1,0:T(8,128)}, u32[]{:S(2)}, u32[]{:S(2)}) collective-permute-start(f32[1536,4096]{1,0:T(8,128)} %fusion.9), channel_id=1, source_target_pairs={{0,1},{1,0},{2,3},{3,2},{4,5},{5,4},{6,7},{7,6}} | collective-permute-start | bytes 75497480 | tf_op jit(solution)/shard_map/ppermute | solution.py:119
  322.3 52.6 %copy-start.2 = (bf16[1,4,1,384,2048]{4,3,2,1,0:T(8,128)(2,1)S(1)}, bf16[1,4,1,384,2048]{4,3,2,1,0:T(8,128)(2,1)}, u32[]{:S(2)}) copy-start(bf16[1,4,1,384,2048]{4,3,2,1,0:T(8,128)(2,1)} %get-tuple-element.70) | copy-start | bytes 18874372
  355.4 19.5 %collective-permute-start.1 = (bf16[1536,4096]{1,0:T(8,128)(2,1)}, bf16[1536,4096]{1,0:T(8,128)(2,1)}, u32[]{:S(2)}, u32[]{:S(2)}) collective-permute-start(bf16[1536,4096]{1,0:T(8,128)(2,1)} %fusion.18), channel_id=1, source_target_pairs={{0,1},{1,0},{2,3},{3,2},{4,5},{5,4},{6,7},{7,6}} | collective-permute-start | bytes 37748744 | tf_op jit(solution)/shard_map/ppermute | solution.py:119
  406.8 337.7 %reduce-scatter.5.cloned.1.call-start = ((), (), s32[]{:S(2)}) async-start(), calls=%async_computation.5 | async-start | bytes 31457280 | tf_op jit(solution)/shard_map/reduce_scatter | solution.py:123
  407.6 493.6 %all-gather.13.cloned.1.call-start = ((), (), s32[]{:S(2)}) async-start(), calls=%async_computation.8 | async-start | bytes 28311552 | tf_op jit(solution)/shard_map/all_gather | solution.py:127
  524.7 473.1 %all-gather.11.cloned.1.call-start = ((), (), s32[]{:S(2)}) async-start(), calls=%async_computation.6 | async-start | bytes 28311552 | tf_op jit(solution)/shard_map/all_gather | solution.py:127
  753.9 378.4 %all-gather.15.cloned.1.call-start = ((), (), s32[]{:S(2)}) async-start(), calls=%async_computation.9 | async-start | bytes 28311552 | tf_op jit(solution)/shard_map/all_gather | solution.py:127
  774.2 422.6 %reduce-scatter.9.cloned.1.call-start = ((), (), s32[]{:S(2)}) async-start(), calls=%async_computation.10 | async-start | bytes 7864320 | tf_op jit(solution)/shard_map/reduce_scatter | solution.py:123
  1091.1 28.2 %slice-start.2 = ((s8[12582912]{0:T(1024)(128)(4,1)}), s8[4194304]{0:T(1024)(128)(4,1)S(1)}, s32[]{:S(2)}) async-start(s8[12582912]{0:T(1024)(128)(4,1)} %bitcast.122), calls=%async_computation.17 | async-start | bytes 8388608
  1094.1 25.2 %slice-start.3 = ((s8[12582912]{0:T(1024)(128)(4,1)}), s8[4194304]{0:T(1024)(128)(4,1)S(1)}, s32[]{:S(2)}) async-start(s8[12582912]{0:T(1024)(128)(4,1)} %bitcast.122), calls=%async_computation.18 | async-start | bytes 8388608
  1094.1 25.2 %slice-start.4 = ((s8[12582912]{0:T(1024)(128)(4,1)}), s8[4194304]{0:T(1024)(128)(4,1)S(1)}, s32[]{:S(2)}) async-start(s8[12582912]{0:T(1024)(128)(4,1)} %bitcast.122), calls=%async_computation.19 | async-start | bytes 8388608
  1108.8 10.5 collective-permute-start.2
  1132.4 259.9 %all-gather.21.cloned.1.call-start = ((), (), s32[]{:S(2)}) async-start(), calls=%async_computation.14 | async-start | bytes 28311552 | tf_op jit(solution)/shard_map/all_gather | solution.py:172
  1240.4 1.6 copy-start
  1242.0 266.4 %reduce-scatter.11.cloned.1.call-start = ((), (), s32[]{:S(2)}) async-start(), calls=%async_computation.11 | async-start | bytes 7864320 | tf_op jit(solution)/shard_map/reduce_scatter | solution.py:123
  1242.1 21.3 %slice-start.5 = ((s8[4718592]{0:T(1024)(128)(4,1)}), s8[4194304]{0:T(1024)(128)(4,1)S(1)}, s32[]{:S(2)}) async-start(s8[4718592]{0:T(1024)(128)(4,1)} %bitcast.132), calls=%async_computation.20 | async-start | bytes 8388608
  1242.1 21.3 %slice-start.7 = ((s8[12582912]{0:T(1024)(128)(4,1)}), s8[4194304]{0:T(1024)(128)(4,1)S(1)}, s32[]{:S(2)}) async-start(s8[12582912]{0:T(1024)(128)(4,1)} %bitcast.145), calls=%async_computation.22 | async-start | bytes 8388608
  1246.4 17.1 %slice-start.6 = ((s8[4718592]{0:T(1024)(128)(4,1)}), s8[524288]{0:T(1024)(128)(4,1)S(1)}, s32[]{:S(2)}) async-start(s8[4718592]{0:T(1024)(128)(4,1)} %bitcast.132), calls=%async_computation.21 | async-start | bytes 1048576
  1246.4 17.1 %slice-start.8 = ((s8[12582912]{0:T(1024)(128)(4,1)}), s8[4194304]{0:T(1024)(128)(4,1)S(1)}, s32[]{:S(2)}) async-start(s8[12582912]{0:T(1024)(128)(4,1)} %bitcast.145), calls=%async_computation.23 | async-start | bytes 8388608
  1246.4 17.1 %slice-start.9 = ((s8[12582912]{0:T(1024)(128)(4,1)}), s8[4194304]{0:T(1024)(128)(4,1)S(1)}, s32[]{:S(2)}) async-start(s8[12582912]{0:T(1024)(128)(4,1)} %bitcast.145), calls=%async_computation.24 | async-start | bytes 8388608
  1263.4 110.5 %collective-permute-start.3 = (bf16[768,4096]{1,0:T(8,128)(2,1)}, bf16[768,4096]{1,0:T(8,128)(2,1)}, u32[]{:S(2)}, u32[]{:S(2)}) collective-permute-start(bf16[768,4096]{1,0:T(8,128)(2,1)} %convolution_convert_fusion.2), channel_id=1, source_target_pairs={{0,1},{1,0},{2,3},{3,2},{4,5},{5,4},{6,7},{7,6}} | collective-permute-start | bytes 18874376 | tf_op jit(solution)/shard_map/ppermute | solution.py:119
  1324.2 28.9 %copy-start.1 = (bf16[3072,512]{1,0:T(8,128)(2,1)S(1)}, bf16[3072,512]{1,0:T(8,128)(2,1)}, u32[]{:S(2)}) copy-start(bf16[3072,512]{1,0:T(8,128)(2,1)} %copy-done) | copy-start | bytes 9437188
  1353.1 20.8 %copy-start.3 = (bf16[1,4,1,192,1536]{4,3,2,1,0:T(8,128)(2,1)S(1)}, bf16[1,4,1,192,1536]{4,3,2,1,0:T(8,128)(2,1)}, u32[]{:S(2)}) copy-start(bf16[1,4,1,192,1536]{4,3,2,1,0:T(8,128)(2,1)} %get-tuple-element.75) | copy-start | bytes 7077892
  1391.6 134.1 %all-gather.19.cloned.1.call-start = ((), (), s32[]{:S(2)}) async-start(), calls=%async_computation.13 | async-start | bytes 14155776 | tf_op jit(solution)/shard_map/all_gather | solution.py:127
  1392.2 201.8 %all-gather.17.cloned.1.call-start = ((), (), s32[]{:S(2)}) async-start(), calls=%async_computation.12 | async-start | bytes 14155776 | tf_op jit(solution)/shard_map/all_gather | solution.py:127
Sparse Core Ops, SparseCore 0:
  9.8 160.1 all-gather.8
  406.9 117.7 reduce-scatter.6
  528.3 216.1 reduce-scatter.4
  746.2 119.6 all-gather.12
  868.1 119.6 all-gather.10
  989.4 119.6 all-gather.14
  1132.5 64.2 reduce-scatter.8
  1242.1 119.6 all-gather.20
  1391.7 65.8 reduce-scatter.10
  1459.2 66.4 all-gather.18
  1527.5 66.4 all-gather.16
